TPU v7x, 256 devices: a whole 4x4x8 slice. The times are simulated.
256 devices in a mesh: gx: 4 (over y_lo, core), gz: 8 (over y_hi, x), ta: 8 (over z).
Axes of the slice: x: 4, y: 4 (y_hi: 2, y_lo: 2; y = y_hi * 2 + y_lo), z: 8, core: 2. Of those that a mesh axis runs over, the one named last changes fastest.
Arguments:
- links: float32 [4, 2, 3, 3, 32, 32, 512], P(None, None, None, None, 'ta', 'gz', 'gx'), may hold values from -1 to 1, as said below
Outputs:
- force: float32 [4, 2, 3, 3, 32, 32, 512], P(None, None, None, None, 'ta', 'gz', 'gx')
Inputs may be any that keep to these rules, and one draw needn't show every extreme that they name: Every link matrix (real part links[mu, 0], imaginary part links[mu, 1]) is special unitary, up to float32 rounding.
All inputs are finite; a program needn't handle non-finite values.
Results may differ from a plain program's by a relative error of at most 0.0003.
Values sent between devices are 32-bit elements; how exact they have to be, the bound alone decides.
No kernel may reach another device: no remote copies, remote signals or barrier semaphores. Data moves between devices by JAX's collectives and lax.ppermute only.
A program may use at most 64 MiB of HBM per device.

v0:
```python
import jax
import jax.numpy as jnp
from jax import lax
from jax.sharding import PartitionSpec as P

NX = 16


COEFF = -1.9


def padded(block, sides, width):
    for axis, dim in sides:
        count = lax.axis_size(axis)
        forward = [(i, i + 1) for i in range(count - 1)]
        forward.append((count - 1, 0))
        backward = [(target, source) for source, target in forward]
        low = lax.ppermute(
            lax.slice_in_dim(block, block.shape[dim] - width, None, axis=dim), axis, forward
        )
        high = lax.ppermute(lax.slice_in_dim(block, 0, width, axis=dim), axis, backward)
        block = jnp.concatenate([low, block, high], axis=dim)
    return block


def matprod(left, right):
    total = left[:, 0][:, None] * right[0][None, :]
    total = total + left[:, 1][:, None] * right[1][None, :]
    return total + left[:, 2][:, None] * right[2][None, :]


def complex_mul(left, right):
    return (
        matprod(left[0], right[0]) - matprod(left[1], right[1]),
        matprod(left[0], right[1]) + matprod(left[1], right[0]),
    )


def dagger(matrix):
    return (jnp.swapaxes(matrix[0], 0, 1), -jnp.swapaxes(matrix[1], 0, 1))


def unit_step(direction, sign):
    offset = [0, 0, 0, 0]
    offset[direction] = sign
    return tuple(offset)


def joined(first_step, second_step):
    return tuple((first_step[position] + second_step[position] for position in range(4)))


def gauge_force(fetch_link):
    blocks = []
    still = (0, 0, 0, 0)
    for direction in range(4):
        ahead = unit_step(direction, 1)
        summed = None
        for transverse in range(4):
            if transverse == direction:
                continue
            side_up = unit_step(transverse, 1)
            side_down = unit_step(transverse, -1)
            upper = complex_mul(
                complex_mul(fetch_link(transverse, ahead), dagger(fetch_link(direction, side_up))),
                dagger(fetch_link(transverse, still)),
            )
            lower = complex_mul(
                complex_mul(
                    dagger(fetch_link(transverse, joined(ahead, side_down))),
                    dagger(fetch_link(direction, side_down)),
                ),
                fetch_link(transverse, side_down),
            )
            staple = (upper[0] + lower[0], upper[1] + lower[1])
            summed = staple if summed is None else (summed[0] + staple[0], summed[1] + staple[1])
        loop_matrix = complex_mul(fetch_link(direction, still), summed)
        real_part = 0.5 * (loop_matrix[0] - jnp.swapaxes(loop_matrix[0], 0, 1))
        imag_part = 0.5 * (loop_matrix[1] + jnp.swapaxes(loop_matrix[1], 0, 1))
        trace_third = (loop_matrix[1][0, 0] + loop_matrix[1][1, 1] + loop_matrix[1][2, 2]) / 3.0
        identity = jnp.eye(3, dtype=jnp.float32).reshape((3, 3) + (1,) * trace_third.ndim)
        imag_part = imag_part - identity * trace_third
        blocks.append(COEFF * jnp.stack([real_part, imag_part], axis=0))
    return jnp.stack(blocks, axis=0)


def complete_rows(wider):
    real0 = wider[:, 0, 0]
    imag0 = wider[:, 1, 0]
    real1 = wider[:, 0, 1]
    imag1 = wider[:, 1, 1]
    real_cols = []
    imag_cols = []
    for column in range(3):
        next_col = (column + 1) % 3
        last_col = (column + 2) % 3
        cross_real = (
            real0[:, next_col] * real1[:, last_col]
            - imag0[:, next_col] * imag1[:, last_col]
            - real0[:, last_col] * real1[:, next_col]
            + imag0[:, last_col] * imag1[:, next_col]
        )
        cross_imag = (
            real0[:, next_col] * imag1[:, last_col]
            + imag0[:, next_col] * real1[:, last_col]
            - real0[:, last_col] * imag1[:, next_col]
            - imag0[:, last_col] * real1[:, next_col]
        )
        real_cols.append(cross_real)
        imag_cols.append(-cross_imag)
    third = jnp.stack([jnp.stack(real_cols, axis=1), jnp.stack(imag_cols, axis=1)], axis=1)
    return jnp.concatenate([wider, third[:, :, None]], axis=2)


def per_device(links):
    payload = links[:, :, 0:2]
    wider = padded(payload, (("gx", 6),), NX)
    wider = padded(wider, (("ta", 4), ("gz", 5)), 1)
    wider = complete_rows(wider)
    time_len = links.shape[4]
    depth_len = links.shape[5]
    flat_len = links.shape[6]
    column = lax.broadcasted_iota(jnp.int32, (flat_len,), 0) % NX
    right_edge = column == NX - 1
    left_edge = column == 0

    def fetch_link(direction, offset):
        start = NX + offset[2] * NX
        field = wider[
            direction,
            :,
            :,
            :,
            1 + offset[0] : 1 + offset[0] + time_len,
            1 + offset[1] : 1 + offset[1] + depth_len,
            start : start + flat_len,
        ]
        if offset[3] == 1:
            field = jnp.where(
                right_edge, jnp.roll(field, NX - 1, axis=5), jnp.roll(field, -1, axis=5)
            )
        elif offset[3] == -1:
            field = jnp.where(
                left_edge, jnp.roll(field, 1 - NX, axis=5), jnp.roll(field, 1, axis=5)
            )
        return (field[0], field[1])

    return gauge_force(fetch_link)


def solution(mesh):
    return jax.shard_map(
        per_device,
        mesh=mesh,
        in_specs=(P(None, None, None, None, "ta", "gz", "gx"),),
        out_specs=P(None, None, None, None, "ta", "gz", "gx"),
        check_vma=False,
    )
```

profile of v0, /device:TPU:14, one launch (start us, length us, event | category | flops | bytes accessed | tf_op | source)
XLA Modules:
  0.0 70.3 jit_solution(11727214759005900719)
XLA Ops:
  0.0 1.4 %fusion.22 = (f32[4,2,2,3,4,4,16]{6,5,4,3,2,1,0:T(4,128)S(1)}, f32[4,2,2,3,4,4,16]{6,5,4,3,2,1,0:T(4,128)S(1)}) fusion(f32[4,2,3,3,4,4,128]{6,5,4,3,2,1,0:T(4,128)} %param.1), kind=kLoop, calls=%fused_computation.729 | loop fusion | bytes 196608 | tf_op jit(solution)/shard_map/slice | solution.py:19
  1.4 0.3 copy.21
  1.8 0.3 copy.19
  2.1 0.6 collective-permute-start
  2.6 0.3 copy.20
  2.9 7.2 %collective-permute-done.1 = f32[4,2,2,3,4,4,16]{6,0,5,4,3,2,1:T(4,128)S(1)} collective-permute-done((f32[4,2,2,3,4,4,16]{6,0,5,4,3,2,1:T(4,128)S(1)}, f32[4,2,2,3,4,4,16]{6,0,5,4,3,2,1:T(4,128)S(1)}, u32[]{:S(2)}, u32[]{:S(2)}) %collective-permute-start.1) | collective-permute-done | bytes 49184 | tf_op jit(solution)/shard_map/ppermute | solution.py:21
  10.1 3.1 %collective-permute-done = f32[4,2,2,3,4,4,16]{6,0,5,4,3,2,1:T(4,128)S(1)} collective-permute-done((f32[4,2,2,3,4,4,16]{6,0,5,4,3,2,1:T(4,128)S(1)}, f32[4,2,2,3,4,4,16]{6,0,5,4,3,2,1:T(4,128)S(1)}, u32[]{:S(2)}, u32[]{:S(2)}) %collective-permute-start) | collective-permute-done | bytes 49184 | tf_op jit(solution)/shard_map/ppermute | solution.py:18
  13.2 0.4 pad_maximum_fusion.10
  13.6 2.0 %collective-permute-start.2 = (f32[4,2,2,3,1,4,160]{6,0,5,4,3,2,1:T(4,128)S(1)}, f32[4,2,2,3,1,4,160]{6,0,5,4,3,2,1:T(4,128)S(1)}, u32[]{:S(2)}, u32[]{:S(2)}) collective-permute-start(f32[4,2,2,3,1,4,160]{6,0,5,4,3,2,1:T(4,128)S(1)} %get-tuple-element.90), channel_id=1, source_target_pairs={{0,1},{1,2},{2,3},{3,4},{4,5},{5,6},{6,7},{7,0},{8,9},{9,10},{10,1... | collective-permute-start | bytes 368648 | tf_op jit(solution)/shard_map/ppermute | solution.py:18
  15.6 4.0 %collective-permute-start.3 = (f32[4,2,2,3,1,4,160]{6,0,5,4,3,2,1:T(4,128)S(1)}, f32[4,2,2,3,1,4,160]{6,0,5,4,3,2,1:T(4,128)S(1)}, u32[]{:S(2)}, u32[]{:S(2)}) collective-permute-start(f32[4,2,2,3,1,4,160]{6,0,5,4,3,2,1:T(4,128)S(1)} %get-tuple-element.91), channel_id=1, source_target_pairs={{1,0},{2,1},{3,2},{4,3},{5,4},{6,5},{7,6},{0,7},{9,8},{10,9},{11,1... | collective-permute-start | bytes 368648 | tf_op jit(solution)/shard_map/ppermute | solution.py:21
  19.6 4.7 %collective-permute-done.2 = f32[4,2,2,3,1,4,160]{6,0,5,4,3,2,1:T(4,128)S(1)} collective-permute-done((f32[4,2,2,3,1,4,160]{6,0,5,4,3,2,1:T(4,128)S(1)}, f32[4,2,2,3,1,4,160]{6,0,5,4,3,2,1:T(4,128)S(1)}, u32[]{:S(2)}, u32[]{:S(2)}) %collective-permute-start.2) | collective-permute-done | bytes 122912 | tf_op jit(solution)/shard_map/ppermute | solution.py:18
  24.4 0.4 pad_maximum_fusion.7
  24.7 2.1 %collective-permute-start.4 = (f32[4,2,2,3,6,1,160]{6,0,5,4,3,2,1:T(4,128)S(1)}, f32[4,2,2,3,6,1,160]{6,0,5,4,3,2,1:T(4,128)S(1)}, u32[]{:S(2)}, u32[]{:S(2)}) collective-permute-start(f32[4,2,2,3,6,1,160]{6,0,5,4,3,2,1:T(4,128)S(1)} %get-tuple-element.84), channel_id=1, source_target_pairs={{0,8},{8,16},{16,24},{24,32},{32,40},{40,48},{48,56},{56,0},{1,9},... | collective-permute-start | bytes 552968 | tf_op jit(solution)/shard_map/ppermute | solution.py:18
  26.9 0.3 pad_maximum_fusion.20
  27.2 5.7 %collective-permute-done.4 = f32[4,2,2,3,6,1,160]{6,0,5,4,3,2,1:T(4,128)S(1)} collective-permute-done((f32[4,2,2,3,6,1,160]{6,0,5,4,3,2,1:T(4,128)S(1)}, f32[4,2,2,3,6,1,160]{6,0,5,4,3,2,1:T(4,128)S(1)}, u32[]{:S(2)}, u32[]{:S(2)}) %collective-permute-start.4) | collective-permute-done | bytes 184352 | tf_op jit(solution)/shard_map/ppermute | solution.py:18
  32.9 5.2 %collective-permute-done.5 = f32[4,2,2,3,6,1,160]{6,0,5,4,3,2,1:T(4,128)S(1)} collective-permute-done((f32[4,2,2,3,6,1,160]{6,0,5,4,3,2,1:T(4,128)S(1)}, f32[4,2,2,3,6,1,160]{6,0,5,4,3,2,1:T(4,128)S(1)}, u32[]{:S(2)}, u32[]{:S(2)}) %collective-permute-start.5) | collective-permute-done | bytes 184352 | tf_op jit(solution)/shard_map/ppermute | solution.py:21
  38.1 1.1 %pad_maximum_fusion.1 = f32[4,2,2,3,6,6,160]{6,0,5,4,3,2,1:T(4,128)S(1)} fusion(f32[4,2,2,3,6,1,160]{6,0,5,4,3,2,1:T(4,128)S(1)} %collective-permute-done.5, f32[4,2,2,3,1,4,160]{6,0,5,4,3,2,1:T(4,128)S(1)} %collective-permute-done.3, f32[4,2,2,3,4,4,16]{6,0,5,4,3,2,1:T(4,128)S(1)} %collective-permute-done.1, f32[4,2,2,3,4,4,128]{6,0,5,4,3,2,1:T(4,128)S(1)} %copy.20, ...), kind=kLoop, calls=%fused_computation.1 | loop fusion | flops 1658880 | bytes 2211840 | tf_op jit(solution)/shard_map/concatenate | solution.py:22
  39.3 0.3 slice_bitcast_fusion.2
  39.6 0.2 multiply_add_fusion.1
  39.8 0.2 multiply_add_fusion.2
  40.0 0.2 subtract_negate_fusion.2
  40.2 0.2 maximum_bitcast_fusion.1
  40.5 0.2 maximum_bitcast_fusion
  40.7 0.3 fusion.21
  41.0 1.5 %pad_maximum_fusion = f32[4,2,3,3,6,6,160]{6,0,5,4,3,2,1:T(4,128)S(1)} fusion(f32[4,2,1,3,6,6,160]{6,0,5,4,3,2,1:T(4,128)S(1)} %maximum_bitcast_fusion, f32[4,2,2,3,6,1,160]{6,0,5,4,3,2,1:T(4,128)S(1)} %collective-permute-done.5, f32[4,2,2,3,1,4,160]{6,0,5,4,3,2,1:T(4,128)S(1)} %collective-permute-done.3, ...), kind=kLoop, calls=%fused_computation | loop fusion | flops 2903040 | bytes 3317760 | tf_op jit(solution)/shard_map/concatenate | solution.py:112
  42.5 2.5 %slice_negate_fusion.23 = (f32[1,1,3,3,4,4,128]{6,0,5,4,3,2,1:T(1,128)S(1)}, f32[1,1,3,3,4,4,128]{6,0,5,4,3,2,1:T(1,128)S(1)}, f32[1,1,3,3,4,4,128]{6,0,5,4,3,2,...) fusion(f32[4,2,3,3,6,6,160]{6,0,5,4,3,2,1:T(4,128)S(1)} %pad_ma, ...), kind=kLoop, calls=%fused_computation.85 | loop fusion | flops 55296 | bytes 2654208 | tf_op jit(solution)/shard_map/neg | solution.py:40
  45.2 2.7 %fusion.18 = (f32[1,1,3,3,4,4,128]{6,0,5,4,3,2,1:T(1,128)S(1)}, f32[1,1,3,3,4,4,128]{6,0,5,4,3,2,1:T(1,128)S(1)}, f32[1,1,3,3,4,4,128]{6,0,5,4,3,2,1:T(1,128)S(1...) fusion(f32[4,2,3,3,6,6,160]{6,0,5,4,3,2,1:T(4,128)S(1)} %pad_ma, ...), kind=kLoop, calls=%fused_computation.725 | loop fusion | flops 147456 | bytes 2801664 | tf_op jit(solution)/shard_map/slice | solution.py:146
  48.0 2.5 %fusion.19 = (f32[1,1,3,3,4,4,128]{6,0,5,4,3,2,1:T(1,128)S(1)}, f32[1,1,3,3,4,4,128]{6,0,5,4,3,2,1:T(1,128)S(1)}, f32[1,1,3,3,4,4,128]{6,0,5,4,3,2,1:T(1,128)S(1...) fusion(f32[4,2,3,3,6,6,160]{6,0,5,4,3,2,1:T(4,128)S(1)} %pad_ma, ...), kind=kLoop, calls=%fused_computation.726 | loop fusion | flops 73728 | bytes 2801664 | tf_op jit(solution)/shard_map/slice | solution.py:146
  50.5 2.9 %fusion.20 = (f32[1,2,3,3,4,4,128]{6,0,5,4,3,2,1:T(1,128)S(1)}, f32[1,2,3,3,4,4,128]{6,0,5,4,3,2,1:T(1,128)S(1)}, f32[1,2,3,3,4,4,128]{6,0,5,4,3,2,1:T(1,128)S(1...) fusion(f32[4,2,3,3,6,6,160]{6,0,5,4,3,2,1:T(4,128)S(1)} %pad_ma, ...), kind=kLoop, calls=%fused_computation.727 | loop fusion | bytes 2949120 | tf_op jit(solution)/shard_map/slice | solution.py:129
  53.8 0.1 slice.4514
  54.0 0.1 slice.4120
  54.3 0.1 slice.4450
  54.8 0.4 slice.4148
  55.9 0.1 fusion.32
  56.0 0.1 fusion.31
  56.2 0.1 fusion.34
  56.3 0.1 fusion.33
  56.5 0.1 fusion.28
  56.6 0.1 fusion.27
  56.8 0.1 fusion.30
  56.9 0.1 fusion.29
  57.1 0.1 fusion.24
  57.2 0.1 fusion.23
  57.4 0.1 fusion.26
  57.5 0.1 fusion.25
  57.7 0.7 maximum_select_fusion
  60.8 0.4 maximum_select_fusion.11
  61.5 0.5 maximum_select_fusion.6
  62.3 0.7 maximum_select_fusion.1
  64.0 0.2 pad_maximum_fusion.28
  64.2 0.3 pad_maximum_fusion.21
  64.5 0.4 add_add_fusion.2
  64.9 0.4 add_add_fusion.1
  65.4 0.4 add_add_fusion.10
  65.9 0.4 add_add_fusion.11
  66.4 0.2 multiply_bitcast_fusion
  66.5 0.2 multiply_bitcast_fusion.1
  66.8 0.4 add_add_fusion.29
  67.2 0.4 add_add_fusion.28
  67.7 0.2 multiply_bitcast_fusion.3
  68.0 0.4 add_add_fusion.20
  68.4 0.4 add_add_fusion.19
  68.9 0.2 multiply_bitcast_fusion.2
  69.3 0.9 %pad_maximum_fusion.2 = f32[4,2,3,3,4,4,128]{6,5,4,3,2,1,0:T(4,128)} fusion(f32[1,2,3,3,4,4,128]{6,5,4,3,2,1,0:T(4,128)S(1)} %maximum_multiply_fusion.3, f32[1,2,3,3,4,4,128]{6,5,4,3,2,1,0:T(4,128)S(1)} %maximum_multiply_fusion.2, f32[1,2,3,3,4,4,128]{6,5,4,3,2,1,0:T(4,128)S(1)} %maximum_multiply_fusion.1, ...), kind=kLoop, calls=%fused_computation.3 | loop fusion | flops 442368 | bytes 1179648 | tf_op jit(solution)/shard_map/stack | solution.py:84
  (251 shorter events, 5.3 us)
Async XLA Ops:
  0.0 2.6 %slice-start = ((f32[4,2,3,3,4,4,128]{6,5,4,3,2,1,0:T(4,128)}), f32[4,2,2,3,4,4,128]{6,5,4,3,2,1,0:T(4,128)S(1)}, s32[]{:S(2)}) async-start(f32[4,2,3,3,4,4,128]{6,5,4,3,2,1,0:T(4,128)} %param.1), calls=%async_computation | async-start | bytes 786432 | tf_op jit(solution)/shard_map/slice | solution.py:116
  1.7 8.4 %collective-permute-start.1 = (f32[4,2,2,3,4,4,16]{6,0,5,4,3,2,1:T(4,128)S(1)}, f32[4,2,2,3,4,4,16]{6,0,5,4,3,2,1:T(4,128)S(1)}, u32[]{:S(2)}, u32[]{:S(2)}) collective-permute-start(f32[4,2,2,3,4,4,16]{6,0,5,4,3,2,1:T(4,128)S(1)} %copy.21), channel_id=1, source_target_pairs={{64,0},{128,64},{192,128},{0,192},{65,1},{129,65},{193,129},{1,193... | collective-permute-start | bytes 147464 | tf_op jit(solution)/shard_map/ppermute | solution.py:21
  2.1 11.2 %collective-permute-start = (f32[4,2,2,3,4,4,16]{6,0,5,4,3,2,1:T(4,128)S(1)}, f32[4,2,2,3,4,4,16]{6,0,5,4,3,2,1:T(4,128)S(1)}, u32[]{:S(2)}, u32[]{:S(2)}) collective-permute-start(f32[4,2,2,3,4,4,16]{6,0,5,4,3,2,1:T(4,128)S(1)} %copy.19), channel_id=1, source_target_pairs={{0,64},{64,128},{128,192},{192,0},{1,65},{65,129},{129,193},{193,1... | collective-permute-start | bytes 147464 | tf_op jit(solution)/shard_map/ppermute | solution.py:18
  13.6 10.8 %collective-permute-start.2 = (f32[4,2,2,3,1,4,160]{6,0,5,4,3,2,1:T(4,128)S(1)}, f32[4,2,2,3,1,4,160]{6,0,5,4,3,2,1:T(4,128)S(1)}, u32[]{:S(2)}, u32[]{:S(2)}) collective-permute-start(f32[4,2,2,3,1,4,160]{6,0,5,4,3,2,1:T(4,128)S(1)} %get-tuple-element.90), channel_id=1, source_target_pairs={{0,1},{1,2},{2,3},{3,4},{4,5},{5,6},{6,7},{7,0},{8,9},{9,10},{10,1... | collective-permute-start | bytes 368648 | tf_op jit(solution)/shard_map/ppermute | solution.py:18
  15.6 8.8 %collective-permute-start.3 = (f32[4,2,2,3,1,4,160]{6,0,5,4,3,2,1:T(4,128)S(1)}, f32[4,2,2,3,1,4,160]{6,0,5,4,3,2,1:T(4,128)S(1)}, u32[]{:S(2)}, u32[]{:S(2)}) collective-permute-start(f32[4,2,2,3,1,4,160]{6,0,5,4,3,2,1:T(4,128)S(1)} %get-tuple-element.91), channel_id=1, source_target_pairs={{1,0},{2,1},{3,2},{4,3},{5,4},{6,5},{7,6},{0,7},{9,8},{10,9},{11,1... | collective-permute-start | bytes 368648 | tf_op jit(solution)/shard_map/ppermute | solution.py:21
  24.7 8.2 %collective-permute-start.4 = (f32[4,2,2,3,6,1,160]{6,0,5,4,3,2,1:T(4,128)S(1)}, f32[4,2,2,3,6,1,160]{6,0,5,4,3,2,1:T(4,128)S(1)}, u32[]{:S(2)}, u32[]{:S(2)}) collective-permute-start(f32[4,2,2,3,6,1,160]{6,0,5,4,3,2,1:T(4,128)S(1)} %get-tuple-element.84), channel_id=1, source_target_pairs={{0,8},{8,16},{16,24},{24,32},{32,40},{40,48},{48,56},{56,0},{1,9},... | collective-permute-start | bytes 552968 | tf_op jit(solution)/shard_map/ppermute | solution.py:18
  26.9 11.3 %collective-permute-start.5 = (f32[4,2,2,3,6,1,160]{6,0,5,4,3,2,1:T(4,128)S(1)}, f32[4,2,2,3,6,1,160]{6,0,5,4,3,2,1:T(4,128)S(1)}, u32[]{:S(2)}, u32[]{:S(2)}) collective-permute-start(f32[4,2,2,3,6,1,160]{6,0,5,4,3,2,1:T(4,128)S(1)} %get-tuple-element.85), channel_id=1, source_target_pairs={{8,0},{16,8},{24,16},{32,24},{40,32},{48,40},{56,48},{0,56},{9,1},... | collective-permute-start | bytes 552968 | tf_op jit(solution)/shard_map/ppermute | solution.py:21
where the time goes:
time: 70.4 us; the launch traced here: 70.3 us
  waiting for transfers between devices  26 us (37%)
  other arithmetic  22.5 us (32%)
  local copies, waits for them, and re-layouts  10.9 us (15%)
  starting transfers between devices  8.8 us (12%)
  between operations  2.04 us (3%)
    ppermute x3, waiting for transfers between devices, padded(): lax.ppermute(lax.slice_in_dim(block, block.shape[dim] - width, None, axis...  13.6 us
    ppermute x3, waiting for transfers between devices, padded(): lax.ppermute(lax.slice_in_dim(block, 0, width, axis=dim), axis, backward)  12.4 us
    slice x2, other arithmetic, fetch_link(): return (field[0], field[1])  5.21 us
    ppermute x3, starting transfers between devices, padded(): lax.ppermute(lax.slice_in_dim(block, block.shape[dim] - width, None, axis...  4.68 us
    ppermute x3, starting transfers between devices, padded(): lax.ppermute(lax.slice_in_dim(block, 0, width, axis=dim), axis, backward)  4.11 us
    slice x1, local copies, waits for them, and re-layouts, fetch_link(): wider[direction, :, :, :, 1 + offset[0]:1 + offset[0] + time_len, 1 + off...  2.89 us
    neg x17, other arithmetic, dagger(): return (jnp.swapaxes(matrix[0], 0, 1), -jnp.swapaxes(matrix[1], 0, 1))  2.77 us
    slice x10, local copies, waits for them, and re-layouts, fetch_link(): jnp.roll(field, 1, axis=5)  1.66 us
  transfers between devices with their start and end apart: 6, of which 5 were waited for; matrix products, arithmetic and copies ran while one was open for 1% of the time, Pallas kernels for 0%

commit v1 on v0

v1 whole, which is shorter than its diff:
```python
import jax
import jax.numpy as jnp
from jax import lax
from jax.experimental import pallas as pl
from jax.experimental.pallas import tpu as pltpu
from jax.sharding import PartitionSpec as P

NX = 16
COEFF = -1.9

ROWS = 16
LANES = 128
TIMES = 4
DEPTHS = 4
PAIRS = ((0, 1), (0, 2), (0, 3), (1, 2), (1, 3), (2, 3))
OTHERS = tuple(tuple(d for d in range(4) if d != face) for face in range(3))


def comp(direction, part, row, col):
    return ((direction * 2 + part) * 3 + row) * 3 + col


def face_comp(slot, part, row, col):
    return ((slot * 2 + part) * 2 + row) * 3 + col


def accumulate(terms):
    total = None
    for sign, left, right in terms:
        product = left * right
        if total is None:
            total = product if sign > 0 else -product
        else:
            total = total + product if sign > 0 else total - product
    return total


def product_rows(left, right):
    out = []
    for row in left:
        cols = []
        for j in range(3):
            re = accumulate(
                [(1, row[k][0], right[k][j][0]) for k in range(3)]
                + [(-1, row[k][1], right[k][j][1]) for k in range(3)]
            )
            im = accumulate(
                [(1, row[k][0], right[k][j][1]) for k in range(3)]
                + [(1, row[k][1], right[k][j][0]) for k in range(3)]
            )
            cols.append((re, im))
        out.append(cols)
    return out


def product_rows_dagger(left, right):
    out = []
    for row in left:
        cols = []
        for j in range(3):
            re = accumulate(
                [(1, row[k][0], right[j][k][0]) for k in range(3)]
                + [(1, row[k][1], right[j][k][1]) for k in range(3)]
            )
            im = accumulate(
                [(1, row[k][1], right[j][k][0]) for k in range(3)]
                + [(-1, row[k][0], right[j][k][1]) for k in range(3)]
            )
            cols.append((re, im))
        out.append(cols)
    return out


def cross_real(row0, row1, j):
    a, b = (j + 1) % 3, (j + 2) % 3
    return accumulate(
        [
            (1, row0[a][0], row1[b][0]),
            (-1, row0[a][1], row1[b][1]),
            (-1, row0[b][0], row1[a][0]),
            (1, row0[b][1], row1[a][1]),
        ]
    )


def cross_imag(row0, row1, j):
    a, b = (j + 1) % 3, (j + 2) % 3
    return accumulate(
        [
            (1, row0[b][0], row1[a][1]),
            (1, row0[b][1], row1[a][0]),
            (-1, row0[a][0], row1[b][1]),
            (-1, row0[a][1], row1[b][0]),
        ]
    )


def third_row(row0, row1):
    return [(cross_real(row0, row1, j), cross_imag(row0, row1, j)) for j in range(3)]


def plaquette(left, left_ahead, right, right_ahead):
    first = product_rows(left[:2], left_ahead)
    second = product_rows(right[:2], right_ahead)
    second.append(third_row(second[0], second[1]))
    loop = product_rows_dagger(first, second)
    row0, row1 = loop
    re20 = cross_real(row0, row1, 0)
    im20 = cross_imag(row0, row1, 0)
    re21 = cross_real(row0, row1, 1)
    im21 = cross_imag(row0, row1, 1)
    im22 = cross_imag(row0, row1, 2)
    third = (row0[0][1] + row1[1][1] + im22) * (1.0 / 3.0)
    d0 = row0[0][1] - third
    d1 = row1[1][1] - third
    return [
        row0[1][0] - row1[0][0],
        row0[1][1] + row1[0][1],
        row0[2][0] - re20,
        row0[2][1] + im20,
        row1[2][0] - re21,
        row1[2][1] + im21,
        d0 + d0,
        d1 + d1,
    ]


def rotated(force, link):
    r01, i01, r02, i02, r12, i12, d0, d1 = force
    d2 = -(d0 + d1)
    diag = (d0, d1, d2)
    upper = {(0, 1): (r01, i01), (0, 2): (r02, i02), (1, 2): (r12, i12)}
    columns = []
    for j in range(3):
        entries = []
        for k in range(3):
            re_terms = [(-1, diag[k], link[k][j][1])]
            im_terms = [(1, diag[k], link[k][j][0])]
            for l in range(3):
                if l == k:
                    continue
                if l > k:
                    re, im = upper[(k, l)]
                    sign = 1
                else:
                    re, im = upper[(l, k)]
                    sign = -1
                re_terms = [(sign, re, link[l][j][0])] + re_terms + [(-1, im, link[l][j][1])]
                im_terms = [(1, im, link[l][j][0])] + im_terms + [(sign, re, link[l][j][1])]
            re_terms.sort(key=lambda term: -term[0])
            entries.append((accumulate(re_terms), accumulate(im_terms)))
        columns.append(entries)

    def real(i, j):
        return accumulate(
            [(1, link[k][i][0], columns[j][k][0]) for k in range(3)]
            + [(1, link[k][i][1], columns[j][k][1]) for k in range(3)]
        )

    def imag(i, j):
        return accumulate(
            [(1, link[k][i][0], columns[j][k][1]) for k in range(3)]
            + [(-1, link[k][i][1], columns[j][k][0]) for k in range(3)]
        )

    return [real(0, 1), imag(0, 1), real(0, 2), imag(0, 2), real(1, 2), imag(1, 2), imag(0, 0), imag(1, 1)]


def lane_group(shape):
    return lax.broadcasted_iota(jnp.int32, shape, 1) // NX


def row_index(shape):
    return lax.broadcasted_iota(jnp.int32, shape, 0)


def turned(value, groups):
    return pltpu.roll(value, groups % 8 * NX, 1) if groups % 8 else value


def packed(values, last):
    total = None
    for group, value in enumerate(values):
        value = turned(value, group + 1 if last else group)
        total = value if total is None else jnp.where(lane_group(value.shape) == group, value, total)
    return total


def unpacked(value, group, last):
    return turned(value, 7 - group if last else -group)


def send_kernel(links, time_out, depth_out, plane_out):
    for face, out in ((0, time_out), (1, depth_out)):
        for slot, direction in enumerate(OTHERS[face]):
            for part in range(2):
                for row in range(2):
                    for col in range(3):
                        source = comp(direction, part, row, col)
                        target = face_comp(slot, part, row, col) * 4
                        if face == 0:
                            out[target : target + 4] = links[source, 0:DEPTHS]
                        else:
                            out[target : target + 4] = links[source, pl.ds(0, TIMES, stride=DEPTHS)]
    for part in range(2):
        for row in range(2):
            for col in range(3):
                target = ((part * 2 + row) * 3 + col) * 8
                plane_out[target : target + 8] = packed(
                    [
                        links[comp(direction, part, row, col), 8 * half : 8 * half + 8]
                        for half in range(2)
                        for direction in OTHERS[2]
                    ],
                    False,
                )


def matrix(ref, base, rows):
    return [
        [(ref[base + row * 3 + col, rows], ref[base + 9 + row * 3 + col, rows]) for col in range(3)]
        for row in range(3)
    ]


def face_matrix(ref, slot, size):
    rows = [
        [
            tuple(
                ref[face_comp(slot, part, row, col) * size : (face_comp(slot, part, row, col) + 1) * size]
                for part in range(2)
            )
            for col in range(3)
        ]
        for row in range(2)
    ]
    rows.append(third_row(rows[0], rows[1]))
    return rows


def shift_links(links, time_in, depth_in, plane_in, shifted):
    column = lax.broadcasted_iota(jnp.int32, (8, LANES), 1) % NX
    right_edge = column == NX - 1
    last_plane = lane_group((8, LANES)) == LANES // NX - 1
    for face in range(2):
        received = time_in if face == 0 else depth_in
        for slot, direction in enumerate(OTHERS[face]):
            halo = face_matrix(received, slot, 4)
            for part in range(2):
                for row in range(3):
                    for col in range(3):
                        c = comp(direction, part, row, col)
                        if face == 0:
                            shifted[0, c, 0 : ROWS - 4] = links[c, 4:ROWS]
                            shifted[0, c, ROWS - 4 : ROWS] = halo[row][col][part]
                        else:
                            shifted[1, c, 0 : ROWS - 1] = links[c, 1:ROWS]
                            shifted[1, c, pl.ds(3, TIMES, stride=DEPTHS)] = halo[row][col][part]
    halo = face_matrix(plane_in, 0, 8)
    for part in range(2):
        for row in range(3):
            for col in range(3):
                for slot, direction in enumerate(OTHERS[2]):
                    c = comp(direction, part, row, col)
                    for half in range(2):
                        rows = slice(8 * half, 8 * half + 8)
                        outer = unpacked(halo[row][col][part], 3 * half + slot, True)
                        shifted[2, c, rows] = jnp.where(last_plane, outer, turned(links[c, rows], 7))
    for direction in range(3):
        for offset in range(18):
            c = direction * 18 + offset
            for half in range(2):
                rows = slice(8 * half, 8 * half + 8)
                value = links[c, rows]
                shifted[3, c, rows] = jnp.where(
                    right_edge, pltpu.roll(value, NX - 1, 1), pltpu.roll(value, LANES - 1, 1)
                )


def main_kernel(
    links, time_in, depth_in, plane_in, force, time_out, depth_out, plane_out, shifted, moved, plane
):
    shift_links(links, time_in, depth_in, plane_in, shifted)
    for face in range(2):
        for c in range(24):
            moved[face, c, 0:8] = jnp.zeros((8, LANES), jnp.float32)

    def step(half, carry):
        start = pl.multiple_of(half * 8, 8)
        rows = pl.ds(start, 8)
        column = lax.broadcasted_iota(jnp.int32, (8, LANES), 1)
        left_edge = column % NX == 0
        first_plane = column < NX
        fresh = [True] * 4

        def add(direction, values, sign):
            for i in range(8):
                c = direction * 8 + i
                if fresh[direction]:
                    force[c, rows] = values[i] if sign > 0 else -values[i]
                elif sign > 0:
                    force[c, rows] = force[c, rows] + values[i]
                else:
                    force[c, rows] = force[c, rows] - values[i]
            fresh[direction] = False

        def carry_over(direction, step_direction, values, sign):
            if step_direction < 2:
                slot = OTHERS[step_direction].index(direction)
                lower = pl.ds(pl.multiple_of(start + 8, 8), 8)
                for i in range(8):
                    moved[step_direction, slot * 8 + i, lower] = values[i] if sign > 0 else -values[i]
                return
            if step_direction == 2:
                slot = OTHERS[2].index(direction)
                for i in range(8):
                    plane[slot * 8 + i, rows] = values[i] if sign > 0 else -values[i]
                values = [jnp.where(first_plane, 0.0, turned(v, 1)) for v in values]
            else:
                values = [
                    jnp.where(left_edge, pltpu.roll(v, LANES - NX + 1, 1), pltpu.roll(v, 1, 1))
                    for v in values
                ]
            add(direction, values, sign)

        for mu, nu in PAIRS:
            link_mu = matrix(links, mu * 18, rows)
            link_nu = matrix(links, nu * 18, rows)
            values = plaquette(
                link_mu,
                matrix(shifted.at[mu], nu * 18, rows),
                link_nu,
                matrix(shifted.at[nu], mu * 18, rows),
            )
            add(mu, values, 1)
            add(nu, values, -1)
            carry_over(mu, nu, rotated(values, link_nu), -1)
            carry_over(nu, mu, rotated(values, link_mu), 1)
        return carry

    lax.fori_loop(0, 2, step, 0)

    inner = row_index((8, LANES)) % DEPTHS != 0
    for direction in range(4):
        for i in range(8):
            c = direction * 8 + i
            for half in range(2):
                rows = slice(8 * half, 8 * half + 8)
                total = force[c, rows]
                if direction != 0:
                    slot = OTHERS[0].index(direction) * 8 + i
                    total = total + moved[0, slot, 8 * half + 4 : 8 * half + 12]
                if direction != 1:
                    slot = OTHERS[1].index(direction) * 8 + i
                    total = total + jnp.where(inner, moved[1, slot, 8 * half + 7 : 8 * half + 15], 0.0)
                force[c, rows] = total
    for c in range(24):
        time_out[4 * c : 4 * c + 4] = moved[0, c, 20:24]
        depth_out[4 * c : 4 * c + 4] = moved[1, c, pl.ds(11, TIMES, stride=DEPTHS)]
    for i in range(8):
        plane_out[8 * i : 8 * i + 8] = packed(
            [plane[slot * 8 + i, 8 * half : 8 * half + 8] for half in range(2) for slot in range(3)], True
        )


def final_kernel(force, time_in, depth_in, plane_in, out, work):
    first_plane = lax.broadcasted_iota(jnp.int32, (8, LANES), 1) < NX
    for direction in range(4):
        for i in range(8):
            c = direction * 8 + i
            for half in range(2):
                rows = slice(8 * half, 8 * half + 8)
                total = force[c, rows]
                if direction != 2:
                    group = 3 * half + OTHERS[2].index(direction)
                    outer = unpacked(plane_in[8 * i : 8 * i + 8], group, False)
                    total = total + jnp.where(first_plane, outer, 0.0)
                work[c, rows] = total
            if direction != 0:
                at = (OTHERS[0].index(direction) * 8 + i) * 4
                work[c, 0:4] = work[c, 0:4] + time_in[at : at + 4]
            if direction != 1:
                at = (OTHERS[1].index(direction) * 8 + i) * 4
                sites = pl.ds(0, TIMES, stride=DEPTHS)
                work[c, sites] = work[c, sites] + depth_in[at : at + 4]
        half_coeff = 0.5 * COEFF
        upper = ((0, 1), (0, 2), (1, 2))
        for half in range(2):
            rows = slice(8 * half, 8 * half + 8)
            for n, (row, col) in enumerate(upper):
                re = work[direction * 8 + 2 * n, rows] * half_coeff
                im = work[direction * 8 + 2 * n + 1, rows] * half_coeff
                out[comp(direction, 0, row, col), rows] = re
                out[comp(direction, 0, col, row), rows] = -re
                out[comp(direction, 1, row, col), rows] = im
                out[comp(direction, 1, col, row), rows] = im
            d0 = work[direction * 8 + 6, rows] * half_coeff
            d1 = work[direction * 8 + 7, rows] * half_coeff
            zero = jnp.zeros_like(d0)
            for k, value in enumerate((d0, d1, -(d0 + d1))):
                out[comp(direction, 1, k, k), rows] = value
                out[comp(direction, 0, k, k), rows] = zero


def shape(*dims):
    return jax.ShapeDtypeStruct(dims, jnp.float32)


def move(value, axis, forward):
    count = lax.axis_size(axis)
    step = 1 if forward else count - 1
    return lax.ppermute(value, axis, [(i, (i + step) % count) for i in range(count)])


def per_device(links):
    flat = links.reshape(72, ROWS, LANES)
    faces = pl.pallas_call(
        send_kernel, out_shape=(shape(144, LANES), shape(144, LANES), shape(96, LANES)), name="send"
    )(flat)
    depth = move(faces[1], "gz", False)
    time = move(faces[0], "ta", False)
    plane = move(faces[2], "gx", False)
    force, time, depth, plane = pl.pallas_call(
        main_kernel,
        out_shape=(shape(32, ROWS, LANES), shape(96, LANES), shape(96, LANES), shape(64, LANES)),
        scratch_shapes=[
            pltpu.VMEM((4, 72, ROWS, LANES), jnp.float32),
            pltpu.VMEM((2, 24, 24, LANES), jnp.float32),
            pltpu.VMEM((24, ROWS, LANES), jnp.float32),
        ],
        name="main",
    )(flat, time, depth, plane)
    depth = move(depth, "gz", True)
    time = move(time, "ta", True)
    plane = move(plane, "gx", True)
    out = pl.pallas_call(
        final_kernel,
        out_shape=shape(72, ROWS, LANES),
        scratch_shapes=[pltpu.VMEM((32, ROWS, LANES), jnp.float32)],
        name="final",
    )(force, time, depth, plane)
    return out.reshape(links.shape)


def solution(mesh):
    spec = P(None, None, None, None, "ta", "gz", "gx")
    return jax.shard_map(per_device, mesh=mesh, in_specs=(spec,), out_specs=spec, check_vma=False)
```

time: 70.4 us -> 32.9 us (0.47)
  the two profiles are of different devices: /device:TPU:14 before, /device:TPU:1 now
where the time goes in v1:
time: 32.9 us; the launch traced here: 32.7 us
  starting transfers between devices  13 us (40%)
  waiting for transfers between devices  9.85 us (30%)
  Pallas kernels  8.02 us (24%)
  local copies, waits for them, and re-layouts  1.88 us (6%)
    ppermute x6, starting transfers between devices, move(): lax.ppermute(value, axis, [(i, (i + step) % count) for i in range(count)])  13 us
    ppermute x6, waiting for transfers between devices, move(): lax.ppermute(value, axis, [(i, (i + step) % count) for i in range(count)])  9.85 us
    pallas_call x1, Pallas kernels, per_device(): pl.pallas_call(main_kernel, out_shape=(shape(32, ROWS, LANES), shape(96,...  4.26 us
    pallas_call x1, Pallas kernels, per_device(): pl.pallas_call(final_kernel, out_shape=shape(72, ROWS, LANES), scratch_sh...  1.94 us
    unnamed x12, local copies, waits for them, and re-layouts  1.88 us
    pallas_call x1, Pallas kernels, per_device(): pl.pallas_call(send_kernel, out_shape=(shape(144, LANES), shape(144, LANE...  1.82 us
  transfers between devices with their start and end apart: 6, of which 4 were waited for; matrix products, arithmetic and copies ran while one was open for 0% of the time, Pallas kernels for 0%

profile of v1, /device:TPU:1, one launch (start us, length us, event | category | flops | bytes accessed | tf_op | source)
XLA Modules:
  0.0 32.7 jit_solution(7066796252952978391)
XLA Ops:
  0.0 1.8 %send.1 = (f32[144,128]{1,0:T(8,128)}, f32[144,128]{1,0:T(8,128)}, f32[96,128]{1,0:T(8,128)}) custom-call(f32[72,16,128]{2,1,0:T(8,128)} %bitcast.2), custom_call_target="tpu_custom_call" | custom-call | tf_op jit(solution)/shard_map/send/pallas_call | solution.py:417
  1.8 6.4 %collective-permute-start = (f32[144,128]{1,0:T(8,128)}, f32[144,128]{1,0:T(8,128)S(1)}, u32[]{:S(2)}, u32[]{:S(2)}) collective-permute-start(f32[144,128]{1,0:T(8,128)} %get-tuple-element.12), channel_id=1, source_target_pairs={{0,7},{1,0},{2,1},{3,2},{4,3},{5,4},{6,5},{7,6},{8,15},{9,8},{10,9... | collective-permute-start | bytes 221192 | tf_op jit(solution)/shard_map/ppermute | solution.py:412
  8.2 5.1 %collective-permute-start.1 = (f32[144,128]{1,0:T(8,128)}, f32[144,128]{1,0:T(8,128)S(1)}, u32[]{:S(2)}, u32[]{:S(2)}) collective-permute-start(f32[144,128]{1,0:T(8,128)} %get-tuple-element.13), channel_id=1, source_target_pairs={{0,56},{8,0},{16,8},{24,16},{32,24},{40,32},{48,40},{56,48},{1,57}... | collective-permute-start | bytes 221192 | tf_op jit(solution)/shard_map/ppermute | solution.py:412
  13.3 1.2 %collective-permute-start.2 = (f32[96,128]{1,0:T(8,128)}, f32[96,128]{1,0:T(8,128)S(1)}, u32[]{:S(2)}, u32[]{:S(2)}) collective-permute-start(f32[96,128]{1,0:T(8,128)} %get-tuple-element.14), channel_id=1, source_target_pairs={{0,192},{64,0},{128,64},{192,128},{1,193},{65,1},{129,65},{193,129... | collective-permute-start | bytes 147464 | tf_op jit(solution)/shard_map/ppermute | solution.py:412
  14.6 2.5 %collective-permute-done.2.plane_in = f32[96,128]{1,0:T(8,128)S(1)} collective-permute-done((f32[96,128]{1,0:T(8,128)}, f32[96,128]{1,0:T(8,128)S(1)}, u32[]{:S(2)}, u32[]{:S(2)}) %collective-permute-start.2) | collective-permute-done | bytes 49184 | tf_op jit(solution)/shard_map/ppermute | solution.py:412
  17.1 0.0 copy-start.2
  17.1 0.0 collective-permute-done.time_in
  17.1 0.0 copy-start
  17.1 0.0 collective-permute-done.1.depth_in
  17.1 0.6 %copy-done.2 = f32[96,128]{1,0:T(8,128)} copy-done((f32[96,128]{1,0:T(8,128)}, f32[96,128]{1,0:T(8,128)S(1)}, u32[]{:S(2)}) %copy-start.2) | copy-done | bytes 49176
  17.7 0.0 copy-done
  17.7 0.0 copy-start.1
  17.7 0.6 %copy-done.1 = f32[144,128]{1,0:T(8,128)} copy-done((f32[144,128]{1,0:T(8,128)}, f32[144,128]{1,0:T(8,128)S(1)}, u32[]{:S(2)}) %copy-start.1) | copy-done | bytes 73752
  18.3 4.3 %main.1 = (f32[32,16,128]{2,1,0:T(8,128)}, f32[96,128]{1,0:T(8,128)}, f32[96,128]{1,0:T(8,128)}, f32[64,128]{1,0:T(8,128)}) custom-call(f32[72,16,128]{2,1,0:T(8,128)} %bitcast.3, f32[144,128]{1,0:T(8,128)} %copy-done, f32[144,128]{1,0:T(8,128)} %copy-done.1, f32[96,128]{1,0:T(8,128)} %copy-done.2), custom_call_target="tpu_custom_call" | custom-call | tf_op jit(solution)/shard_map/main/pallas_call | solution.py:423
  22.6 0.0 collective-permute-start.3
  22.6 0.1 collective-permute-start.4
  22.7 0.2 collective-permute-start.5
  22.8 1.3 %collective-permute-done.5.plane_in = f32[64,128]{1,0:T(8,128)S(1)} collective-permute-done((f32[64,128]{1,0:T(8,128)}, f32[64,128]{1,0:T(8,128)S(1)}, u32[]{:S(2)}, u32[]{:S(2)}) %collective-permute-start.5) | collective-permute-done | bytes 32800 | tf_op jit(solution)/shard_map/ppermute | solution.py:412
  24.2 0.0 copy-start.5
  24.2 3.6 %collective-permute-done.3.time_in = f32[96,128]{1,0:T(8,128)S(1)} collective-permute-done((f32[96,128]{1,0:T(8,128)}, f32[96,128]{1,0:T(8,128)S(1)}, u32[]{:S(2)}, u32[]{:S(2)}) %collective-permute-start.3) | collective-permute-done | bytes 49184 | tf_op jit(solution)/shard_map/ppermute | solution.py:412
  27.7 0.0 copy-start.3
  27.7 2.5 %collective-permute-done.4.depth_in = f32[96,128]{1,0:T(8,128)S(1)} collective-permute-done((f32[96,128]{1,0:T(8,128)}, f32[96,128]{1,0:T(8,128)S(1)}, u32[]{:S(2)}, u32[]{:S(2)}) %collective-permute-start.4) | collective-permute-done | bytes 49184 | tf_op jit(solution)/shard_map/ppermute | solution.py:412
  30.2 0.0 copy-start.4
  30.2 0.0 copy-done.5
  30.2 0.0 copy-done.3
  30.2 0.6 %copy-done.4 = f32[96,128]{1,0:T(8,128)} copy-done((f32[96,128]{1,0:T(8,128)}, f32[96,128]{1,0:T(8,128)S(1)}, u32[]{:S(2)}) %copy-start.4) | copy-done | bytes 49176
  30.8 1.9 %final.1 = f32[72,16,128]{2,1,0:T(8,128)} custom-call(f32[32,16,128]{2,1,0:T(8,128)} %get-tuple-element.15.force, f32[96,128]{1,0:T(8,128)} %copy-done.3, f32[96,128]{1,0:T(8,128)} %copy-done.4, f32[64,128]{1,0:T(8,128)} %copy-done.5), custom_call_target="tpu_custom_call" | custom-call | tf_op jit(solution)/shard_map/final/pallas_call | solution.py:436
Async XLA Ops:
  1.8 15.2 %collective-permute-start = (f32[144,128]{1,0:T(8,128)}, f32[144,128]{1,0:T(8,128)S(1)}, u32[]{:S(2)}, u32[]{:S(2)}) collective-permute-start(f32[144,128]{1,0:T(8,128)} %get-tuple-element.12), channel_id=1, source_target_pairs={{0,7},{1,0},{2,1},{3,2},{4,3},{5,4},{6,5},{7,6},{8,15},{9,8},{10,9... | collective-permute-start | bytes 221192 | tf_op jit(solution)/shard_map/ppermute | solution.py:412
  8.2 8.8 %collective-permute-start.1 = (f32[144,128]{1,0:T(8,128)}, f32[144,128]{1,0:T(8,128)S(1)}, u32[]{:S(2)}, u32[]{:S(2)}) collective-permute-start(f32[144,128]{1,0:T(8,128)} %get-tuple-element.13), channel_id=1, source_target_pairs={{0,56},{8,0},{16,8},{24,16},{32,24},{40,32},{48,40},{56,48},{1,57}... | collective-permute-start | bytes 221192 | tf_op jit(solution)/shard_map/ppermute | solution.py:412
  13.3 3.7 %collective-permute-start.2 = (f32[96,128]{1,0:T(8,128)}, f32[96,128]{1,0:T(8,128)S(1)}, u32[]{:S(2)}, u32[]{:S(2)}) collective-permute-start(f32[96,128]{1,0:T(8,128)} %get-tuple-element.14), channel_id=1, source_target_pairs={{0,192},{64,0},{128,64},{192,128},{1,193},{65,1},{129,65},{193,129... | collective-permute-start | bytes 147464 | tf_op jit(solution)/shard_map/ppermute | solution.py:412
  17.1 0.6 %copy-start.2 = (f32[96,128]{1,0:T(8,128)}, f32[96,128]{1,0:T(8,128)S(1)}, u32[]{:S(2)}) copy-start(f32[96,128]{1,0:T(8,128)S(1)} %collective-permute-done.2.plane_in) | copy-start | bytes 147460
  17.1 0.6 %copy-start = (f32[144,128]{1,0:T(8,128)}, f32[144,128]{1,0:T(8,128)S(1)}, u32[]{:S(2)}) copy-start(f32[144,128]{1,0:T(8,128)S(1)} %collective-permute-done.time_in) | copy-start | bytes 221188
  17.7 0.6 %copy-start.1 = (f32[144,128]{1,0:T(8,128)}, f32[144,128]{1,0:T(8,128)S(1)}, u32[]{:S(2)}) copy-start(f32[144,128]{1,0:T(8,128)S(1)} %collective-permute-done.1.depth_in) | copy-start | bytes 221188
  22.6 5.1 %collective-permute-start.3 = (f32[96,128]{1,0:T(8,128)}, f32[96,128]{1,0:T(8,128)S(1)}, u32[]{:S(2)}, u32[]{:S(2)}) collective-permute-start(f32[96,128]{1,0:T(8,128)} %get-tuple-element.16), channel_id=1, source_target_pairs={{0,1},{1,2},{2,3},{3,4},{4,5},{5,6},{6,7},{7,0},{8,9},{9,10},{10,1... | collective-permute-start | bytes 147464 | tf_op jit(solution)/shard_map/ppermute | solution.py:412
  22.6 7.6 %collective-permute-start.4 = (f32[96,128]{1,0:T(8,128)}, f32[96,128]{1,0:T(8,128)S(1)}, u32[]{:S(2)}, u32[]{:S(2)}) collective-permute-start(f32[96,128]{1,0:T(8,128)} %get-tuple-element.17), channel_id=1, source_target_pairs={{0,8},{8,16},{16,24},{24,32},{32,40},{40,48},{48,56},{56,0},{1,9},... | collective-permute-start | bytes 147464 | tf_op jit(solution)/shard_map/ppermute | solution.py:412
  22.7 1.5 %collective-permute-start.5 = (f32[64,128]{1,0:T(8,128)}, f32[64,128]{1,0:T(8,128)S(1)}, u32[]{:S(2)}, u32[]{:S(2)}) collective-permute-start(f32[64,128]{1,0:T(8,128)} %get-tuple-element.18), channel_id=1, source_target_pairs={{0,64},{64,128},{128,192},{192,0},{1,65},{65,129},{129,193},{193,1... | collective-permute-start | bytes 98312 | tf_op jit(solution)/shard_map/ppermute | solution.py:412
  24.2 6.0 %copy-start.5 = (f32[64,128]{1,0:T(8,128)}, f32[64,128]{1,0:T(8,128)S(1)}, u32[]{:S(2)}) copy-start(f32[64,128]{1,0:T(8,128)S(1)} %collective-permute-done.5.plane_in) | copy-start | bytes 98308
  27.7 2.5 %copy-start.3 = (f32[96,128]{1,0:T(8,128)}, f32[96,128]{1,0:T(8,128)S(1)}, u32[]{:S(2)}) copy-start(f32[96,128]{1,0:T(8,128)S(1)} %collective-permute-done.3.time_in) | copy-start | bytes 147460
  30.2 0.6 %copy-start.4 = (f32[96,128]{1,0:T(8,128)}, f32[96,128]{1,0:T(8,128)S(1)}, u32[]{:S(2)}) copy-start(f32[96,128]{1,0:T(8,128)S(1)} %collective-permute-done.4.depth_in) | copy-start | bytes 147460

commit v2 on v1

--- a/solution.py
+++ b/solution.py
@@ -403,17 +403,18 @@
 
 
 def shape(*dims):
-    return jax.ShapeDtypeStruct(dims, jnp.float32)
+    return pltpu.VMEM(dims, jnp.float32)
 
 
 def move(value, axis, forward):
     count = lax.axis_size(axis)
     step = 1 if forward else count - 1
-    return lax.ppermute(value, axis, [(i, (i + step) % count) for i in range(count)])
+    moved = lax.ppermute(value, axis, [(i, (i + step) % count) for i in range(count)])
+    return pltpu.with_memory_space_constraint(moved, pltpu.VMEM)
 
 
 def per_device(links):
-    flat = links.reshape(72, ROWS, LANES)
+    flat = pltpu.with_memory_space_constraint(links.reshape(72, ROWS, LANES), pltpu.VMEM)
     faces = pl.pallas_call(
         send_kernel, out_shape=(shape(144, LANES), shape(144, LANES), shape(96, LANES)), name="send"
     )(flat)
@@ -435,10 +436,10 @@
     plane = move(plane, "gx", True)
     out = pl.pallas_call(
         final_kernel,
-        out_shape=shape(72, ROWS, LANES),
+        out_shape=jax.ShapeDtypeStruct((72, ROWS, LANES), jnp.float32),
         scratch_shapes=[pltpu.VMEM((32, ROWS, LANES), jnp.float32)],
         name="final",
-    )(force, time, depth, plane)
+    )(pltpu.with_memory_space_constraint(force, pltpu.VMEM), time, depth, plane)
     return out.reshape(links.shape)
 
 

time: 32.9 us -> 26.8 us (0.81)
  Pallas kernels: 8.02 us -> 3.49 us
  local copies, waits for them, and re-layouts: 1.88 us -> 1.06 us
  waiting for transfers between devices: 9.85 us -> 9.05 us
    pallas_call x1, Pallas kernels: 4.26 us -> 2.4 us  [per_device(): pl.pallas_call(main_kernel, out_shape=(shape(32, ROWS, LANES), shape(96,...]
    pallas_call x1, Pallas kernels: 1.82 us -> 0.12 us  [per_device(): pl.pallas_call(send_kernel, out_shape=(shape(144, LANES), shape(144, LANE...]
    pallas_call x1, Pallas kernels: 1.94 us -> 0.96 us  [per_device(): pl.pallas_call(final_kernel, out_shape=jax.ShapeDtypeStruct((72, ROWS, LA...]
    unnamed x12 -> x2, local copies, waits for them, and re-layouts: 1.88 us -> 1.06 us
    ppermute x6, waiting for transfers between devices: 9.85 us -> 9.05 us  [move(): lax.ppermute(value, axis, [(i, (i + step) % count) for i in range(count)])]
where the time goes in v2:
time: 26.8 us; the launch traced here: 26.7 us
  starting transfers between devices  13.1 us (49%)
  waiting for transfers between devices  9.05 us (34%)
  Pallas kernels  3.49 us (13%)
  local copies, waits for them, and re-layouts  1.06 us (4%)
    ppermute x6, starting transfers between devices, move(): lax.ppermute(value, axis, [(i, (i + step) % count) for i in range(count)])  13.1 us
    ppermute x6, waiting for transfers between devices, move(): lax.ppermute(value, axis, [(i, (i + step) % count) for i in range(count)])  9.05 us
    pallas_call x1, Pallas kernels, per_device(): pl.pallas_call(main_kernel, out_shape=(shape(32, ROWS, LANES), shape(96,...  2.4 us
    unnamed x2, local copies, waits for them, and re-layouts  1.06 us
    pallas_call x1, Pallas kernels, per_device(): pl.pallas_call(final_kernel, out_shape=jax.ShapeDtypeStruct((72, ROWS, LA...  0.96 us
  transfers between devices with their start and end apart: 6, of which 4 were waited for; matrix products, arithmetic and copies ran while one was open for 0% of the time, Pallas kernels for 0%

profile of v2, /device:TPU:1, one launch (start us, length us, event | category | flops | bytes accessed | tf_op | source)
XLA Modules:
  0.0 26.7 jit_solution(17115249577341954535)
XLA Ops:
  0.0 0.0 copy-start
  0.0 1.1 %copy-done = f32[4,2,3,3,4,4,128]{6,5,4,3,2,1,0:T(4,128)S(1)} copy-done((f32[4,2,3,3,4,4,128]{6,5,4,3,2,1,0:T(4,128)S(1)}, f32[4,2,3,3,4,4,128]{6,5,4,3,2,1,0:T(4,128)}, u32[]{:S(2)}) %copy-start) | copy-done | bytes 589848
  1.1 0.1 send.1
  1.2 6.5 %collective-permute-start = (f32[144,128]{1,0:T(8,128)S(1)}, f32[144,128]{1,0:T(8,128)S(1)}, u32[]{:S(2)}, u32[]{:S(2)}) collective-permute-start(f32[144,128]{1,0:T(8,128)S(1)} %get-tuple-element.12), channel_id=1, source_target_pairs={{0,7},{1,0},{2,1},{3,2},{4,3},{5,4},{6,5},{7,6},{8,15},{9,8},{10,9... | collective-permute-start | bytes 221192 | tf_op jit(solution)/shard_map/ppermute | solution.py:412
  7.7 5.1 %collective-permute-start.1 = (f32[144,128]{1,0:T(8,128)S(1)}, f32[144,128]{1,0:T(8,128)S(1)}, u32[]{:S(2)}, u32[]{:S(2)}) collective-permute-start(f32[144,128]{1,0:T(8,128)S(1)} %get-tuple-element.13), channel_id=1, source_target_pairs={{0,56},{8,0},{16,8},{24,16},{32,24},{40,32},{48,40},{56,48},{1,57}... | collective-permute-start | bytes 221192 | tf_op jit(solution)/shard_map/ppermute | solution.py:412
  12.8 1.2 %collective-permute-start.2 = (f32[96,128]{1,0:T(8,128)S(1)}, f32[96,128]{1,0:T(8,128)S(1)}, u32[]{:S(2)}, u32[]{:S(2)}) collective-permute-start(f32[96,128]{1,0:T(8,128)S(1)} %get-tuple-element.14), channel_id=1, source_target_pairs={{0,192},{64,0},{128,64},{192,128},{1,193},{65,1},{129,65},{193,129... | collective-permute-start | bytes 147464 | tf_op jit(solution)/shard_map/ppermute | solution.py:412
  14.0 2.3 %collective-permute-done.2.plane_in = f32[96,128]{1,0:T(8,128)S(1)} collective-permute-done((f32[96,128]{1,0:T(8,128)S(1)}, f32[96,128]{1,0:T(8,128)S(1)}, u32[]{:S(2)}, u32[]{:S(2)}) %collective-permute-start.2) | collective-permute-done | bytes 49184 | tf_op jit(solution)/shard_map/ppermute | solution.py:412
  16.3 0.0 collective-permute-done.time_in
  16.3 0.0 collective-permute-done.1.depth_in
  16.3 2.4 %main.1 = (f32[32,16,128]{2,1,0:T(8,128)S(1)}, f32[96,128]{1,0:T(8,128)S(1)}, f32[96,128]{1,0:T(8,128)S(1)}, f32[64,128]{1,0:T(8,128)S(1)}) custom-call(f32[72,16,128]{2,1,0:T(8,128)S(1)} %bitcast.3, f32[144,128]{1,0:T(8,128)S(1)} %collective-permute-done.time_in, f32[144,128]{1,0:T(8,128)S(1)} %collective-permute-done.1.depth_in, ...), custom_call_target="tpu_custom_call" | custom-call | tf_op jit(solution)/shard_map/main/pallas_call | solution.py:424
  18.7 0.1 collective-permute-start.3
  18.8 0.1 collective-permute-start.4
  18.9 0.1 collective-permute-start.5
  19.0 1.2 %collective-permute-done.5.plane_in = f32[64,128]{1,0:T(8,128)S(1)} collective-permute-done((f32[64,128]{1,0:T(8,128)S(1)}, f32[64,128]{1,0:T(8,128)S(1)}, u32[]{:S(2)}, u32[]{:S(2)}) %collective-permute-start.5) | collective-permute-done | bytes 32800 | tf_op jit(solution)/shard_map/ppermute | solution.py:412
  20.2 3.4 %collective-permute-done.3.time_in = f32[96,128]{1,0:T(8,128)S(1)} collective-permute-done((f32[96,128]{1,0:T(8,128)S(1)}, f32[96,128]{1,0:T(8,128)S(1)}, u32[]{:S(2)}, u32[]{:S(2)}) %collective-permute-start.3) | collective-permute-done | bytes 49184 | tf_op jit(solution)/shard_map/ppermute | solution.py:412
  23.6 2.1 %collective-permute-done.4.depth_in = f32[96,128]{1,0:T(8,128)S(1)} collective-permute-done((f32[96,128]{1,0:T(8,128)S(1)}, f32[96,128]{1,0:T(8,128)S(1)}, u32[]{:S(2)}, u32[]{:S(2)}) %collective-permute-start.4) | collective-permute-done | bytes 49184 | tf_op jit(solution)/shard_map/ppermute | solution.py:412
  25.7 1.0 %final.1 = f32[72,16,128]{2,1,0:T(8,128)} custom-call(f32[32,16,128]{2,1,0:T(8,128)S(1)} %get-tuple-element.15.force, f32[96,128]{1,0:T(8,128)S(1)} %collective-permute-done.3.time_in, f32[96,128]{1,0:T(8,128)S(1)} %collective-permute-done.4.depth_in, f32[64,128]{1,0:T(8,128)S(1)} %collective-permute-done.5.plane_in), custom_call_target="tpu_custom_call" | custom-call | tf_op jit(solution)/shard_map/final/pallas_call | solution.py:437
Async XLA Ops:
  0.0 1.1 %copy-start = (f32[4,2,3,3,4,4,128]{6,5,4,3,2,1,0:T(4,128)S(1)}, f32[4,2,3,3,4,4,128]{6,5,4,3,2,1,0:T(4,128)}, u32[]{:S(2)}) copy-start(f32[4,2,3,3,4,4,128]{6,5,4,3,2,1,0:T(4,128)} %param.1) | copy-start | bytes 1769476
  1.2 15.1 %collective-permute-start = (f32[144,128]{1,0:T(8,128)S(1)}, f32[144,128]{1,0:T(8,128)S(1)}, u32[]{:S(2)}, u32[]{:S(2)}) collective-permute-start(f32[144,128]{1,0:T(8,128)S(1)} %get-tuple-element.12), channel_id=1, source_target_pairs={{0,7},{1,0},{2,1},{3,2},{4,3},{5,4},{6,5},{7,6},{8,15},{9,8},{10,9... | collective-permute-start | bytes 221192 | tf_op jit(solution)/shard_map/ppermute | solution.py:412
  7.7 8.6 %collective-permute-start.1 = (f32[144,128]{1,0:T(8,128)S(1)}, f32[144,128]{1,0:T(8,128)S(1)}, u32[]{:S(2)}, u32[]{:S(2)}) collective-permute-start(f32[144,128]{1,0:T(8,128)S(1)} %get-tuple-element.13), channel_id=1, source_target_pairs={{0,56},{8,0},{16,8},{24,16},{32,24},{40,32},{48,40},{56,48},{1,57}... | collective-permute-start | bytes 221192 | tf_op jit(solution)/shard_map/ppermute | solution.py:412
  12.8 3.5 %collective-permute-start.2 = (f32[96,128]{1,0:T(8,128)S(1)}, f32[96,128]{1,0:T(8,128)S(1)}, u32[]{:S(2)}, u32[]{:S(2)}) collective-permute-start(f32[96,128]{1,0:T(8,128)S(1)} %get-tuple-element.14), channel_id=1, source_target_pairs={{0,192},{64,0},{128,64},{192,128},{1,193},{65,1},{129,65},{193,129... | collective-permute-start | bytes 147464 | tf_op jit(solution)/shard_map/ppermute | solution.py:412
  18.7 4.9 %collective-permute-start.3 = (f32[96,128]{1,0:T(8,128)S(1)}, f32[96,128]{1,0:T(8,128)S(1)}, u32[]{:S(2)}, u32[]{:S(2)}) collective-permute-start(f32[96,128]{1,0:T(8,128)S(1)} %get-tuple-element.16), channel_id=1, source_target_pairs={{0,1},{1,2},{2,3},{3,4},{4,5},{5,6},{6,7},{7,0},{8,9},{9,10},{10,1... | collective-permute-start | bytes 147464 | tf_op jit(solution)/shard_map/ppermute | solution.py:412
  18.8 6.9 %collective-permute-start.4 = (f32[96,128]{1,0:T(8,128)S(1)}, f32[96,128]{1,0:T(8,128)S(1)}, u32[]{:S(2)}, u32[]{:S(2)}) collective-permute-start(f32[96,128]{1,0:T(8,128)S(1)} %get-tuple-element.17), channel_id=1, source_target_pairs={{0,8},{8,16},{16,24},{24,32},{32,40},{40,48},{48,56},{56,0},{1,9},... | collective-permute-start | bytes 147464 | tf_op jit(solution)/shard_map/ppermute | solution.py:412
  18.9 1.3 %collective-permute-start.5 = (f32[64,128]{1,0:T(8,128)S(1)}, f32[64,128]{1,0:T(8,128)S(1)}, u32[]{:S(2)}, u32[]{:S(2)}) collective-permute-start(f32[64,128]{1,0:T(8,128)S(1)} %get-tuple-element.18), channel_id=1, source_target_pairs={{0,64},{64,128},{128,192},{192,0},{1,65},{65,129},{129,193},{193,1... | collective-permute-start | bytes 98312 | tf_op jit(solution)/shard_map/ppermute | solution.py:412

commit v3 on v2

--- a/solution.py
+++ b/solution.py
@@ -4,6 +4,7 @@
 from jax.experimental import pallas as pl
 from jax.experimental.pallas import tpu as pltpu
 from jax.sharding import PartitionSpec as P
+
 
 NX = 16
 COEFF = -1.9
@@ -277,9 +278,7 @@
                 )
 
 
-def main_kernel(
-    links, time_in, depth_in, plane_in, force, time_out, depth_out, plane_out, shifted, moved, plane
-):
+def interior_kernel(links, time_in, depth_in, plane_in, force, shifted, moved):
     shift_links(links, time_in, depth_in, plane_in, shifted)
     for face in range(2):
         for c in range(24):
@@ -312,9 +311,6 @@
                     moved[step_direction, slot * 8 + i, lower] = values[i] if sign > 0 else -values[i]
                 return
             if step_direction == 2:
-                slot = OTHERS[2].index(direction)
-                for i in range(8):
-                    plane[slot * 8 + i, rows] = values[i] if sign > 0 else -values[i]
                 values = [jnp.where(first_plane, 0.0, turned(v, 1)) for v in values]
             else:
                 values = [
@@ -354,13 +350,129 @@
                     slot = OTHERS[1].index(direction) * 8 + i
                     total = total + jnp.where(inner, moved[1, slot, 8 * half + 7 : 8 * half + 15], 0.0)
                 force[c, rows] = total
-    for c in range(24):
-        time_out[4 * c : 4 * c + 4] = moved[0, c, 20:24]
-        depth_out[4 * c : 4 * c + 4] = moved[1, c, pl.ds(11, TIMES, stride=DEPTHS)]
-    for i in range(8):
-        plane_out[8 * i : 8 * i + 8] = packed(
-            [plane[slot * 8 + i, 8 * half : 8 * half + 8] for half in range(2) for slot in range(3)], True
+
+
+def cells():
+    return [(part, row, col) for part in range(2) for row in range(2) for col in range(3)]
+
+
+def top(ref, face, c):
+    return ref[c, 12:16] if face == 0 else ref[c, pl.ds(3, TIMES, stride=DEPTHS)]
+
+
+def x_ahead(value):
+    right_edge = lax.broadcasted_iota(jnp.int32, value.shape, 1) % NX == NX - 1
+    return jnp.where(right_edge, pltpu.roll(value, NX - 1, 1), pltpu.roll(value, LANES - 1, 1))
+
+
+def prepare_kernel(links, left, ahead, base):
+    for part in range(2):
+        for row in range(3):
+            for col in range(3):
+                at = part * 9 + row * 3 + col
+                base[0, at, 0:4] = top(links, 0, comp(0, part, row, col))
+                base[0, at, 4:8] = top(links, 1, comp(1, part, row, col))
+                c = comp(2, part, row, col)
+                base[1, at] = packed([links[c, 8 * (q // 3) : 8 * (q // 3) + 8] for q in range(6)], True)
+    for part, row, col in cells():
+        at = face_comp(0, part, row, col)
+        whole = part * 9 + row * 3 + col
+        for unit in range(3):
+            for face in range(2):
+                source = comp(OTHERS[face][unit], part, row, col)
+                left[unit, at, 4 * face : 4 * face + 4] = top(links, face, source)
+        left[3, at] = packed(
+            [
+                links[comp(direction, part, row, col), 8 * half : 8 * half + 8]
+                for half in range(2)
+                for direction in OTHERS[2]
+            ],
+            True,
         )
+        ahead[0, at] = jnp.zeros((8, LANES), jnp.float32)
+        ahead[0, at, 0:3] = links[comp(0, part, row, col), 13:16]
+        ahead[0, at, 4:7] = links[comp(1, part, row, col), pl.ds(7, 3, stride=DEPTHS)]
+        ahead[1, at] = turned(base[0, whole], 7)
+        ahead[2, at] = x_ahead(base[0, whole])
+        c = comp(2, part, row, col)
+        upper = links[c, 8:16]
+        along_x = x_ahead(base[1, whole])
+        group = lane_group((8, LANES))
+        for q, value in (
+            (0, links[c, 4:12]),
+            (1, links[c, 1:9]),
+            (3, pltpu.roll(upper, 4, 0)),
+            (4, pltpu.roll(upper, 7, 0)),
+        ):
+            along_x = jnp.where(group == q, turned(value, q + 1), along_x)
+        ahead[3, at] = along_x
+
+
+def wide(ref, row):
+    return jnp.broadcast_to(ref[row : row + 1], (8, LANES))
+
+
+def boundary_kernel(left, ahead, base, time_in, depth_in, plane_in, time_out, depth_out, plane_out):
+    row_at = row_index((8, LANES))
+    group = lane_group((8, LANES))
+
+    def behind(unit, part, row, col):
+        if unit == 3:
+            at = face_comp(0, part, row, col) * 8
+            return plane_in[at : at + 8]
+        at = face_comp(unit, part, row, col) * 4
+        return jnp.concatenate([time_in[at : at + 4], depth_in[at : at + 4]], axis=0)
+
+    def beside(unit, part, row, col):
+        at = face_comp(0, part, row, col)
+        own = ahead[unit, at]
+        if unit == 0:
+            own = jnp.where(row_at == 3, wide(depth_in, at * 4 + 3), own)
+            return jnp.where(row_at == 7, wide(time_in, at * 4 + 3), own)
+        if unit == 1:
+            time_part = turned(pltpu.roll(plane_in[at * 8 : at * 8 + 8], 4, 0), 4)
+            depth_part = jnp.where(row_at % 2 == 1, wide(plane_in, at * 8 + 7), wide(plane_in, at * 8 + 3))
+            depth_part = jnp.where(row_at < 6, turned(depth_part, 6), turned(depth_part, 3))
+            return jnp.where(group == 7, jnp.where(row_at < 4, time_part, depth_part), own)
+        if unit == 2:
+            return own
+        source = face_comp(1, part, row, col) * 4
+        later = turned(time_in[source - 4 : source + 4], 4)
+        own = jnp.where((group == 3) & (row_at >= 4), later, own)
+        for half in range(2):
+            first, second = wide(depth_in, source + 2 * half), wide(depth_in, source + 2 * half + 1)
+            q = 3 * half + 1
+            deeper = turned(jnp.where(row_at < 4, first, second), q + 1)
+            own = jnp.where((group == q) & (row_at % 4 == 3), deeper, own)
+        return own
+
+    def complete(fetch):
+        rows = [[(fetch(0, row, col), fetch(1, row, col)) for col in range(3)] for row in range(2)]
+        rows.append(third_row(rows[0], rows[1]))
+        return rows
+
+    for unit in range(4):
+        own_base = [
+            [tuple(base[unit // 3, part * 9 + row * 3 + col] for part in range(2)) for col in range(3)]
+            for row in range(3)
+        ]
+        own_left = [
+            [tuple(left[unit, face_comp(0, part, row, col)] for part in range(2)) for col in range(3)]
+            for row in range(2)
+        ]
+        values = plaquette(
+            own_left,
+            complete(lambda part, row, col: beside(unit, part, row, col)),
+            own_base,
+            complete(lambda part, row, col: behind(unit, part, row, col)),
+        )
+        for i, value in enumerate(rotated(values, own_base)):
+            if unit == 3:
+                plane_out[8 * i : 8 * i + 8] = value
+            else:
+                at = (unit * 8 + i) * 4
+                time_out[at : at + 4] = value[0:4]
+                depth_out[at : at + 4] = value[4:8]
 
 
 def final_kernel(force, time_in, depth_in, plane_in, out, work):
@@ -374,15 +486,15 @@
                 if direction != 2:
                     group = 3 * half + OTHERS[2].index(direction)
                     outer = unpacked(plane_in[8 * i : 8 * i + 8], group, False)
-                    total = total + jnp.where(first_plane, outer, 0.0)
+                    total = total - jnp.where(first_plane, outer, 0.0)
                 work[c, rows] = total
             if direction != 0:
                 at = (OTHERS[0].index(direction) * 8 + i) * 4
-                work[c, 0:4] = work[c, 0:4] + time_in[at : at + 4]
+                work[c, 0:4] = work[c, 0:4] - time_in[at : at + 4]
             if direction != 1:
                 at = (OTHERS[1].index(direction) * 8 + i) * 4
                 sites = pl.ds(0, TIMES, stride=DEPTHS)
-                work[c, sites] = work[c, sites] + depth_in[at : at + 4]
+                work[c, sites] = work[c, sites] - depth_in[at : at + 4]
         half_coeff = 0.5 * COEFF
         upper = ((0, 1), (0, 2), (1, 2))
         for half in range(2):
@@ -413,7 +525,7 @@
     return pltpu.with_memory_space_constraint(moved, pltpu.VMEM)
 
 
-def per_device(links):
+def gauge_force(links):
     flat = pltpu.with_memory_space_constraint(links.reshape(72, ROWS, LANES), pltpu.VMEM)
     faces = pl.pallas_call(
         send_kernel, out_shape=(shape(144, LANES), shape(144, LANES), shape(96, LANES)), name="send"
@@ -421,19 +533,29 @@
     depth = move(faces[1], "gz", False)
     time = move(faces[0], "ta", False)
     plane = move(faces[2], "gx", False)
-    force, time, depth, plane = pl.pallas_call(
-        main_kernel,
-        out_shape=(shape(32, ROWS, LANES), shape(96, LANES), shape(96, LANES), shape(64, LANES)),
+    local = pl.pallas_call(
+        prepare_kernel,
+        out_shape=(shape(4, 12, 8, LANES), shape(4, 12, 8, LANES), shape(2, 18, 8, LANES)),
+        name="prepare",
+    )(flat)
+    local = [pltpu.with_memory_space_constraint(value, pltpu.VMEM) for value in local]
+    sent = pl.pallas_call(
+        boundary_kernel,
+        out_shape=(shape(96, LANES), shape(96, LANES), shape(64, LANES)),
+        name="boundary",
+    )(*local, time, depth, plane)
+    force = pl.pallas_call(
+        interior_kernel,
+        out_shape=shape(32, ROWS, LANES),
         scratch_shapes=[
             pltpu.VMEM((4, 72, ROWS, LANES), jnp.float32),
             pltpu.VMEM((2, 24, 24, LANES), jnp.float32),
-            pltpu.VMEM((24, ROWS, LANES), jnp.float32),
         ],
-        name="main",
+        name="interior",
     )(flat, time, depth, plane)
-    depth = move(depth, "gz", True)
-    time = move(time, "ta", True)
-    plane = move(plane, "gx", True)
+    depth = move(sent[1], "gz", True)
+    time = move(sent[0], "ta", True)
+    plane = move(sent[2], "gx", True)
     out = pl.pallas_call(
         final_kernel,
         out_shape=jax.ShapeDtypeStruct((72, ROWS, LANES), jnp.float32),
@@ -445,4 +567,4 @@
 
 def solution(mesh):
     spec = P(None, None, None, None, "ta", "gz", "gx")
-    return jax.shard_map(per_device, mesh=mesh, in_specs=(spec,), out_specs=spec, check_vma=False)
+    return jax.shard_map(gauge_force, mesh=mesh, in_specs=(spec,), out_specs=spec, check_vma=False)

time: 26.8 us -> 25 us (0.933)
  waiting for transfers between devices: 9.05 us -> 6.3 us
  Pallas kernels: 3.49 us -> 4.35 us
    ppermute x6, waiting for transfers between devices: 9.05 us -> 6.3 us  [move(): lax.ppermute(value, axis, [(i, (i + step) % count) for i in range(count)])]
    pallas_call x3 -> x5, Pallas kernels: 3.49 us -> 4.35 us  [the longest x1 2.36 us: gauge_force(): pl.pallas_call(interior_kernel, out_shape=shape(32, ROWS, LANES), scratch...]
    unnamed x2 -> x4, local copies, waits for them, and re-layouts: 1.06 us -> 1.07 us
  transfers between devices with their start and end apart: 6 -> 6, of which waited for: 4 -> 3; matrix products, arithmetic and copies ran while one was open for 0% -> 0% of each run, Pallas kernels for 0% -> 11%
where the time goes in v3:
time: 25 us; the launch traced here: 24.8 us
  starting transfers between devices  13.1 us (52%)
  waiting for transfers between devices  6.3 us (25%)
  Pallas kernels  4.35 us (17%)
  local copies, waits for them, and re-layouts  1.07 us (4%)
    ppermute x6, starting transfers between devices, move(): lax.ppermute(value, axis, [(i, (i + step) % count) for i in range(count)])  13.1 us
    ppermute x6, waiting for transfers between devices, move(): lax.ppermute(value, axis, [(i, (i + step) % count) for i in range(count)])  6.3 us
    pallas_call x1, Pallas kernels, gauge_force(): pl.pallas_call(interior_kernel, out_shape=shape(32, ROWS, LANES), scratch...  2.36 us
    unnamed x4, local copies, waits for them, and re-layouts  1.07 us
    pallas_call x1, Pallas kernels, gauge_force(): pl.pallas_call(final_kernel, out_shape=jax.ShapeDtypeStruct((72, ROWS, LA...  0.96 us
    pallas_call x1, Pallas kernels, gauge_force(): pl.pallas_call(boundary_kernel, out_shape=(shape(96, LANES), shape(96, LA...  0.54 us
  transfers between devices with their start and end apart: 6, of which 3 were waited for; matrix products, arithmetic and copies ran while one was open for 0% of the time, Pallas kernels for 11%

profile of v3, /device:TPU:1, one launch (start us, length us, event | category | flops | bytes accessed | tf_op | source)
XLA Modules:
  0.0 24.8 jit_solution(15505565185932644155)
XLA Ops:
  0.0 0.0 copy-start
  0.0 1.1 %copy-done = f32[4,2,3,3,4,4,128]{6,5,4,3,2,1,0:T(4,128)S(1)} copy-done((f32[4,2,3,3,4,4,128]{6,5,4,3,2,1,0:T(4,128)S(1)}, f32[4,2,3,3,4,4,128]{6,5,4,3,2,1,0:T(4,128)}, u32[]{:S(2)}) %copy-start) | copy-done | bytes 589848
  1.1 0.1 send.1
  1.2 6.5 %collective-permute-start = (f32[144,128]{1,0:T(8,128)S(1)}, f32[144,128]{1,0:T(8,128)S(1)}, u32[]{:S(2)}, u32[]{:S(2)}) collective-permute-start(f32[144,128]{1,0:T(8,128)S(1)} %get-tuple-element.14), channel_id=1, source_target_pairs={{0,7},{1,0},{2,1},{3,2},{4,3},{5,4},{6,5},{7,6},{8,15},{9,8},{10,9... | collective-permute-start | bytes 221192 | tf_op jit(solution)/shard_map/ppermute | solution.py:524
  7.7 5.1 %collective-permute-start.1 = (f32[144,128]{1,0:T(8,128)S(1)}, f32[144,128]{1,0:T(8,128)S(1)}, u32[]{:S(2)}, u32[]{:S(2)}) collective-permute-start(f32[144,128]{1,0:T(8,128)S(1)} %get-tuple-element.15), channel_id=1, source_target_pairs={{0,56},{8,0},{16,8},{24,16},{32,24},{40,32},{48,40},{56,48},{1,57}... | collective-permute-start | bytes 221192 | tf_op jit(solution)/shard_map/ppermute | solution.py:524
  12.8 0.0 copy-start.1
  12.8 1.2 %collective-permute-start.2 = (f32[96,128]{1,0:T(8,128)S(1)}, f32[96,128]{1,0:T(8,128)S(1)}, u32[]{:S(2)}, u32[]{:S(2)}) collective-permute-start(f32[96,128]{1,0:T(8,128)S(1)} %get-tuple-element.16), channel_id=1, source_target_pairs={{0,192},{64,0},{128,64},{192,128},{1,193},{65,1},{129,65},{193,129... | collective-permute-start | bytes 147464 | tf_op jit(solution)/shard_map/ppermute | solution.py:524
  14.0 0.4 %prepare.1 = (f32[4,12,8,128]{3,2,1,0:T(8,128)S(1)}, f32[4,12,8,128]{3,2,1,0:T(8,128)S(1)}, f32[2,18,8,128]{3,2,1,0:T(8,128)S(1)}) custom-call(f32[72,16,128]{2,1,0:T(8,128)S(1)} %bitcast.3), custom_call_target="tpu_custom_call" | custom-call | tf_op jit(solution)/shard_map/prepare/pallas_call | solution.py:536
  14.4 1.9 %collective-permute-done.2.plane_in = f32[96,128]{1,0:T(8,128)S(1)} collective-permute-done((f32[96,128]{1,0:T(8,128)S(1)}, f32[96,128]{1,0:T(8,128)S(1)}, u32[]{:S(2)}, u32[]{:S(2)}) %collective-permute-start.2) | collective-permute-done | bytes 49184 | tf_op jit(solution)/shard_map/ppermute | solution.py:524
  16.3 0.0 collective-permute-done.time_in
  16.3 0.0 collective-permute-done.1.depth_in
  16.3 0.5 %boundary.1 = (f32[96,128]{1,0:T(8,128)S(1)}, f32[96,128]{1,0:T(8,128)S(1)}, f32[64,128]{1,0:T(8,128)S(1)}) custom-call(f32[4,12,8,128]{3,2,1,0:T(8,128)S(1)} %get-tuple-element.17.left, f32[4,12,8,128]{3,2,1,0:T(8,128)S(1)} %get-tuple-element.18.ahead, f32[2,18,8,128]{3,2,1,0:T(8,128)S(1)} %get-tuple-element.19.base, ...), custom_call_target="tpu_custom_call" | custom-call | tf_op jit(solution)/shard_map/boundary/pallas_call | solution.py:542
  16.8 0.1 collective-permute-start.3
  16.9 0.1 collective-permute-start.4
  17.0 0.1 collective-permute-start.5
  17.1 0.0 copy-done.1
  17.1 2.4 %interior.1.force = f32[32,16,128]{2,1,0:T(8,128)S(1)} custom-call(f32[72,16,128]{2,1,0:T(8,128)S(1)} %bitcast.4, f32[144,128]{1,0:T(8,128)S(1)} %collective-permute-done.time_in, f32[144,128]{1,0:T(8,128)S(1)} %collective-permute-done.1.depth_in, f32[96,128]{1,0:T(8,128)S(1)} %collective-permute-done.2.plane_in), custom_call_target="tpu_custom_call" | custom-call | tf_op jit(solution)/shard_map/interior/pallas_call | solution.py:547
  19.5 0.0 collective-permute-done.5.plane_in
  19.5 2.2 %collective-permute-done.3.time_in = f32[96,128]{1,0:T(8,128)S(1)} collective-permute-done((f32[96,128]{1,0:T(8,128)S(1)}, f32[96,128]{1,0:T(8,128)S(1)}, u32[]{:S(2)}, u32[]{:S(2)}) %collective-permute-start.3) | collective-permute-done | bytes 49184 | tf_op jit(solution)/shard_map/ppermute | solution.py:524
  21.7 2.1 %collective-permute-done.4.depth_in = f32[96,128]{1,0:T(8,128)S(1)} collective-permute-done((f32[96,128]{1,0:T(8,128)S(1)}, f32[96,128]{1,0:T(8,128)S(1)}, u32[]{:S(2)}, u32[]{:S(2)}) %collective-permute-start.4) | collective-permute-done | bytes 49184 | tf_op jit(solution)/shard_map/ppermute | solution.py:524
  23.9 1.0 %final.1 = f32[72,16,128]{2,1,0:T(8,128)} custom-call(f32[32,16,128]{2,1,0:T(8,128)S(1)} %interior.1.force, f32[96,128]{1,0:T(8,128)S(1)} %collective-permute-done.3.time_in, f32[96,128]{1,0:T(8,128)S(1)} %collective-permute-done.4.depth_in, f32[64,128]{1,0:T(8,128)S(1)} %collective-permute-done.5.plane_in), custom_call_target="tpu_custom_call" | custom-call | tf_op jit(solution)/shard_map/final/pallas_call | solution.py:559
Async XLA Ops:
  0.0 1.1 %copy-start = (f32[4,2,3,3,4,4,128]{6,5,4,3,2,1,0:T(4,128)S(1)}, f32[4,2,3,3,4,4,128]{6,5,4,3,2,1,0:T(4,128)}, u32[]{:S(2)}) copy-start(f32[4,2,3,3,4,4,128]{6,5,4,3,2,1,0:T(4,128)} %param.1) | copy-start | bytes 1769476
  1.2 15.1 %collective-permute-start = (f32[144,128]{1,0:T(8,128)S(1)}, f32[144,128]{1,0:T(8,128)S(1)}, u32[]{:S(2)}, u32[]{:S(2)}) collective-permute-start(f32[144,128]{1,0:T(8,128)S(1)} %get-tuple-element.14), channel_id=1, source_target_pairs={{0,7},{1,0},{2,1},{3,2},{4,3},{5,4},{6,5},{7,6},{8,15},{9,8},{10,9... | collective-permute-start | bytes 221192 | tf_op jit(solution)/shard_map/ppermute | solution.py:524
  7.7 8.6 %collective-permute-start.1 = (f32[144,128]{1,0:T(8,128)S(1)}, f32[144,128]{1,0:T(8,128)S(1)}, u32[]{:S(2)}, u32[]{:S(2)}) collective-permute-start(f32[144,128]{1,0:T(8,128)S(1)} %get-tuple-element.15), channel_id=1, source_target_pairs={{0,56},{8,0},{16,8},{24,16},{32,24},{40,32},{48,40},{56,48},{1,57}... | collective-permute-start | bytes 221192 | tf_op jit(solution)/shard_map/ppermute | solution.py:524
  12.8 4.3 %copy-start.1 = (f32[4,2,3,3,4,4,128]{6,5,4,3,2,1,0:T(4,128)S(1)}, f32[4,2,3,3,4,4,128]{6,5,4,3,2,1,0:T(4,128)}, u32[]{:S(2)}) copy-start(f32[4,2,3,3,4,4,128]{6,5,4,3,2,1,0:T(4,128)} %param.1) | copy-start | bytes 1769476
  12.8 3.5 %collective-permute-start.2 = (f32[96,128]{1,0:T(8,128)S(1)}, f32[96,128]{1,0:T(8,128)S(1)}, u32[]{:S(2)}, u32[]{:S(2)}) collective-permute-start(f32[96,128]{1,0:T(8,128)S(1)} %get-tuple-element.16), channel_id=1, source_target_pairs={{0,192},{64,0},{128,64},{192,128},{1,193},{65,1},{129,65},{193,129... | collective-permute-start | bytes 147464 | tf_op jit(solution)/shard_map/ppermute | solution.py:524
  16.8 4.9 %collective-permute-start.3 = (f32[96,128]{1,0:T(8,128)S(1)}, f32[96,128]{1,0:T(8,128)S(1)}, u32[]{:S(2)}, u32[]{:S(2)}) collective-permute-start(f32[96,128]{1,0:T(8,128)S(1)} %get-tuple-element.20), channel_id=1, source_target_pairs={{0,1},{1,2},{2,3},{3,4},{4,5},{5,6},{6,7},{7,0},{8,9},{9,10},{10,1... | collective-permute-start | bytes 147464 | tf_op jit(solution)/shard_map/ppermute | solution.py:524
  16.9 6.9 %collective-permute-start.4 = (f32[96,128]{1,0:T(8,128)S(1)}, f32[96,128]{1,0:T(8,128)S(1)}, u32[]{:S(2)}, u32[]{:S(2)}) collective-permute-start(f32[96,128]{1,0:T(8,128)S(1)} %get-tuple-element.21), channel_id=1, source_target_pairs={{0,8},{8,16},{16,24},{24,32},{32,40},{40,48},{48,56},{56,0},{1,9},... | collective-permute-start | bytes 147464 | tf_op jit(solution)/shard_map/ppermute | solution.py:524
  17.0 2.5 %collective-permute-start.5 = (f32[64,128]{1,0:T(8,128)S(1)}, f32[64,128]{1,0:T(8,128)S(1)}, u32[]{:S(2)}, u32[]{:S(2)}) collective-permute-start(f32[64,128]{1,0:T(8,128)S(1)} %get-tuple-element.22), channel_id=1, source_target_pairs={{0,64},{64,128},{128,192},{192,0},{1,65},{65,129},{129,193},{193,1... | collective-permute-start | bytes 98312 | tf_op jit(solution)/shard_map/ppermute | solution.py:524

commit v4 on v3

--- a/solution.py
+++ b/solution.py
@@ -412,7 +412,15 @@
     return jnp.broadcast_to(ref[row : row + 1], (8, LANES))
 
 
-def boundary_kernel(left, ahead, base, time_in, depth_in, plane_in, time_out, depth_out, plane_out):
+def faces_kernel(left, ahead, base, time_in, depth_in, plane_in, time_out, depth_out):
+    boundary((0, 1, 2), left, ahead, base, time_in, depth_in, plane_in, time_out, depth_out, None)
+
+
+def plane_kernel(left, ahead, base, time_in, depth_in, plane_in, plane_out):
+    boundary((3,), left, ahead, base, time_in, depth_in, plane_in, None, None, plane_out)
+
+
+def boundary(units, left, ahead, base, time_in, depth_in, plane_in, time_out, depth_out, plane_out):
     row_at = row_index((8, LANES))
     group = lane_group((8, LANES))
 
@@ -451,7 +459,7 @@
         rows.append(third_row(rows[0], rows[1]))
         return rows
 
-    for unit in range(4):
+    for unit in units:
         own_base = [
             [tuple(base[unit // 3, part * 9 + row * 3 + col] for part in range(2)) for col in range(3)]
             for row in range(3)
@@ -539,11 +547,12 @@
         name="prepare",
     )(flat)
     local = [pltpu.with_memory_space_constraint(value, pltpu.VMEM) for value in local]
-    sent = pl.pallas_call(
-        boundary_kernel,
-        out_shape=(shape(96, LANES), shape(96, LANES), shape(64, LANES)),
-        name="boundary",
-    )(*local, time, depth, plane)
+    sent = pl.pallas_call(faces_kernel, out_shape=(shape(96, LANES), shape(96, LANES)), name="faces")(
+        *local, time, depth, plane
+    )
+    sent_plane = pl.pallas_call(plane_kernel, out_shape=shape(64, LANES), name="plane")(
+        *local, time, depth, plane
+    )
     force = pl.pallas_call(
         interior_kernel,
         out_shape=shape(32, ROWS, LANES),
@@ -555,7 +564,7 @@
     )(flat, time, depth, plane)
     depth = move(sent[1], "gz", True)
     time = move(sent[0], "ta", True)
-    plane = move(sent[2], "gx", True)
+    plane = move(sent_plane, "gx", True)
     out = pl.pallas_call(
         final_kernel,
         out_shape=jax.ShapeDtypeStruct((72, ROWS, LANES), jnp.float32),

time: 25 us -> 24.9 us (level)
  waiting for transfers between devices: 6.3 us -> 5.94 us
    ppermute x6, waiting for transfers between devices: 6.3 us -> 5.94 us  [move(): lax.ppermute(value, axis, [(i, (i + step) % count) for i in range(count)])]
    pallas_call x1 -> x2, Pallas kernels: 0.54 us -> 0.59 us  [the longest x1 0.41 us: gauge_force(): pl.pallas_call(faces_kernel, out_shape=(shape(96, LANES), shape(96, LANES...]
  transfers between devices with their start and end apart: 6 -> 6, of which waited for: 3 -> 3; matrix products, arithmetic and copies ran while one was open for 0% -> 0% of each run, Pallas kernels for 11% -> 12%
where the time goes in v4:
time: 24.9 us; the launch traced here: 24.7 us
  starting transfers between devices  13.1 us (53%)
  waiting for transfers between devices  5.94 us (24%)
  Pallas kernels  4.4 us (18%)
  local copies, waits for them, and re-layouts  1.25 us (5%)
    ppermute x6, starting transfers between devices, move(): lax.ppermute(value, axis, [(i, (i + step) % count) for i in range(count)])  13.1 us
    ppermute x6, waiting for transfers between devices, move(): lax.ppermute(value, axis, [(i, (i + step) % count) for i in range(count)])  5.94 us
    pallas_call x1, Pallas kernels, gauge_force(): pl.pallas_call(interior_kernel, out_shape=shape(32, ROWS, LANES), scratch...  2.36 us
    unnamed x4, local copies, waits for them, and re-layouts  1.25 us
    pallas_call x1, Pallas kernels, gauge_force(): pl.pallas_call(final_kernel, out_shape=jax.ShapeDtypeStruct((72, ROWS, LA...  0.96 us
  transfers between devices with their start and end apart: 6, of which 3 were waited for; matrix products, arithmetic and copies ran while one was open for 0% of the time, Pallas kernels for 12%

profile of v4, /device:TPU:1, one launch (start us, length us, event | category | flops | bytes accessed | tf_op | source)
XLA Modules:
  0.0 24.7 jit_solution(7561593158688307506)
XLA Ops:
  0.0 0.0 copy-start
  0.0 1.1 %copy-done = f32[4,2,3,3,4,4,128]{6,5,4,3,2,1,0:T(4,128)S(1)} copy-done((f32[4,2,3,3,4,4,128]{6,5,4,3,2,1,0:T(4,128)S(1)}, f32[4,2,3,3,4,4,128]{6,5,4,3,2,1,0:T(4,128)}, u32[]{:S(2)}) %copy-start) | copy-done | bytes 589848
  1.1 0.1 send.1
  1.2 6.5 %collective-permute-start = (f32[144,128]{1,0:T(8,128)S(1)}, f32[144,128]{1,0:T(8,128)S(1)}, u32[]{:S(2)}, u32[]{:S(2)}) collective-permute-start(f32[144,128]{1,0:T(8,128)S(1)} %get-tuple-element.13), channel_id=1, source_target_pairs={{0,7},{1,0},{2,1},{3,2},{4,3},{5,4},{6,5},{7,6},{8,15},{9,8},{10,9... | collective-permute-start | bytes 221192 | tf_op jit(solution)/shard_map/ppermute | solution.py:532
  7.7 5.1 %collective-permute-start.1 = (f32[144,128]{1,0:T(8,128)S(1)}, f32[144,128]{1,0:T(8,128)S(1)}, u32[]{:S(2)}, u32[]{:S(2)}) collective-permute-start(f32[144,128]{1,0:T(8,128)S(1)} %get-tuple-element.14), channel_id=1, source_target_pairs={{0,56},{8,0},{16,8},{24,16},{32,24},{40,32},{48,40},{56,48},{1,57}... | collective-permute-start | bytes 221192 | tf_op jit(solution)/shard_map/ppermute | solution.py:532
  12.8 1.2 %collective-permute-start.2 = (f32[96,128]{1,0:T(8,128)S(1)}, f32[96,128]{1,0:T(8,128)S(1)}, u32[]{:S(2)}, u32[]{:S(2)}) collective-permute-start(f32[96,128]{1,0:T(8,128)S(1)} %get-tuple-element.15), channel_id=1, source_target_pairs={{0,192},{64,0},{128,64},{192,128},{1,193},{65,1},{129,65},{193,129... | collective-permute-start | bytes 147464 | tf_op jit(solution)/shard_map/ppermute | solution.py:532
  14.0 0.4 %prepare.1 = (f32[4,12,8,128]{3,2,1,0:T(8,128)S(1)}, f32[4,12,8,128]{3,2,1,0:T(8,128)S(1)}, f32[2,18,8,128]{3,2,1,0:T(8,128)S(1)}) custom-call(f32[72,16,128]{2,1,0:T(8,128)S(1)} %bitcast.3), custom_call_target="tpu_custom_call" | custom-call | tf_op jit(solution)/shard_map/prepare/pallas_call | solution.py:544
  14.4 1.9 %collective-permute-done.2.plane_in = f32[96,128]{1,0:T(8,128)S(1)} collective-permute-done((f32[96,128]{1,0:T(8,128)S(1)}, f32[96,128]{1,0:T(8,128)S(1)}, u32[]{:S(2)}, u32[]{:S(2)}) %collective-permute-start.2) | collective-permute-done | bytes 49184 | tf_op jit(solution)/shard_map/ppermute | solution.py:532
  16.3 0.0 collective-permute-done.time_in
  16.3 0.0 collective-permute-done.1.depth_in
  16.3 0.0 copy-start.1
  16.3 0.4 %faces.1 = (f32[96,128]{1,0:T(8,128)S(1)}, f32[96,128]{1,0:T(8,128)S(1)}) custom-call(f32[4,12,8,128]{3,2,1,0:T(8,128)S(1)} %get-tuple-element.16.left, f32[4,12,8,128]{3,2,1,0:T(8,128)S(1)} %get-tuple-element.17.ahead, f32[2,18,8,128]{3,2,1,0:T(8,128)S(1)} %get-tuple-element.18.base, f32[144,128]{1,0:T(8,128)S(1)} %collective-permute-done.time_in, ...), custom_call_target="tpu_custom_call" | custom-call | tf_op jit(solution)/shard_map/faces/pallas_call | solution.py:550
  16.7 0.1 collective-permute-start.3
  16.8 0.1 collective-permute-start.4
  16.9 0.2 plane.1
  17.1 0.1 collective-permute-start.5
  17.2 0.2 copy-done.1
  17.4 2.4 %interior.1.force = f32[32,16,128]{2,1,0:T(8,128)S(1)} custom-call(f32[72,16,128]{2,1,0:T(8,128)S(1)} %bitcast.4, f32[144,128]{1,0:T(8,128)S(1)} %collective-permute-done.time_in, f32[144,128]{1,0:T(8,128)S(1)} %collective-permute-done.1.depth_in, f32[96,128]{1,0:T(8,128)S(1)} %collective-permute-done.2.plane_in), custom_call_target="tpu_custom_call" | custom-call | tf_op jit(solution)/shard_map/interior/pallas_call | solution.py:556
  19.7 0.0 collective-permute-done.5.plane_in
  19.7 1.9 %collective-permute-done.3.time_in = f32[96,128]{1,0:T(8,128)S(1)} collective-permute-done((f32[96,128]{1,0:T(8,128)S(1)}, f32[96,128]{1,0:T(8,128)S(1)}, u32[]{:S(2)}, u32[]{:S(2)}) %collective-permute-start.3) | collective-permute-done | bytes 49184 | tf_op jit(solution)/shard_map/ppermute | solution.py:532
  21.6 2.1 %collective-permute-done.4.depth_in = f32[96,128]{1,0:T(8,128)S(1)} collective-permute-done((f32[96,128]{1,0:T(8,128)S(1)}, f32[96,128]{1,0:T(8,128)S(1)}, u32[]{:S(2)}, u32[]{:S(2)}) %collective-permute-start.4) | collective-permute-done | bytes 49184 | tf_op jit(solution)/shard_map/ppermute | solution.py:532
  23.8 1.0 %final.1 = f32[72,16,128]{2,1,0:T(8,128)} custom-call(f32[32,16,128]{2,1,0:T(8,128)S(1)} %interior.1.force, f32[96,128]{1,0:T(8,128)S(1)} %collective-permute-done.3.time_in, f32[96,128]{1,0:T(8,128)S(1)} %collective-permute-done.4.depth_in, f32[64,128]{1,0:T(8,128)S(1)} %collective-permute-done.5.plane_in), custom_call_target="tpu_custom_call" | custom-call | tf_op jit(solution)/shard_map/final/pallas_call | solution.py:568
Async XLA Ops:
  0.0 1.1 %copy-start = (f32[4,2,3,3,4,4,128]{6,5,4,3,2,1,0:T(4,128)S(1)}, f32[4,2,3,3,4,4,128]{6,5,4,3,2,1,0:T(4,128)}, u32[]{:S(2)}) copy-start(f32[4,2,3,3,4,4,128]{6,5,4,3,2,1,0:T(4,128)} %param.1) | copy-start | bytes 1769476
  1.2 15.1 %collective-permute-start = (f32[144,128]{1,0:T(8,128)S(1)}, f32[144,128]{1,0:T(8,128)S(1)}, u32[]{:S(2)}, u32[]{:S(2)}) collective-permute-start(f32[144,128]{1,0:T(8,128)S(1)} %get-tuple-element.13), channel_id=1, source_target_pairs={{0,7},{1,0},{2,1},{3,2},{4,3},{5,4},{6,5},{7,6},{8,15},{9,8},{10,9... | collective-permute-start | bytes 221192 | tf_op jit(solution)/shard_map/ppermute | solution.py:532
  7.7 8.6 %collective-permute-start.1 = (f32[144,128]{1,0:T(8,128)S(1)}, f32[144,128]{1,0:T(8,128)S(1)}, u32[]{:S(2)}, u32[]{:S(2)}) collective-permute-start(f32[144,128]{1,0:T(8,128)S(1)} %get-tuple-element.14), channel_id=1, source_target_pairs={{0,56},{8,0},{16,8},{24,16},{32,24},{40,32},{48,40},{56,48},{1,57}... | collective-permute-start | bytes 221192 | tf_op jit(solution)/shard_map/ppermute | solution.py:532
  12.8 3.5 %collective-permute-start.2 = (f32[96,128]{1,0:T(8,128)S(1)}, f32[96,128]{1,0:T(8,128)S(1)}, u32[]{:S(2)}, u32[]{:S(2)}) collective-permute-start(f32[96,128]{1,0:T(8,128)S(1)} %get-tuple-element.15), channel_id=1, source_target_pairs={{0,192},{64,0},{128,64},{192,128},{1,193},{65,1},{129,65},{193,129... | collective-permute-start | bytes 147464 | tf_op jit(solution)/shard_map/ppermute | solution.py:532
  16.3 1.1 %copy-start.1 = (f32[4,2,3,3,4,4,128]{6,5,4,3,2,1,0:T(4,128)S(1)}, f32[4,2,3,3,4,4,128]{6,5,4,3,2,1,0:T(4,128)}, u32[]{:S(2)}) copy-start(f32[4,2,3,3,4,4,128]{6,5,4,3,2,1,0:T(4,128)} %param.1) | copy-start | bytes 1769476
  16.7 4.9 %collective-permute-start.3 = (f32[96,128]{1,0:T(8,128)S(1)}, f32[96,128]{1,0:T(8,128)S(1)}, u32[]{:S(2)}, u32[]{:S(2)}) collective-permute-start(f32[96,128]{1,0:T(8,128)S(1)} %get-tuple-element.19), channel_id=1, source_target_pairs={{0,1},{1,2},{2,3},{3,4},{4,5},{5,6},{6,7},{7,0},{8,9},{9,10},{10,1... | collective-permute-start | bytes 147464 | tf_op jit(solution)/shard_map/ppermute | solution.py:532
  16.8 6.9 %collective-permute-start.4 = (f32[96,128]{1,0:T(8,128)S(1)}, f32[96,128]{1,0:T(8,128)S(1)}, u32[]{:S(2)}, u32[]{:S(2)}) collective-permute-start(f32[96,128]{1,0:T(8,128)S(1)} %get-tuple-element.20), channel_id=1, source_target_pairs={{0,8},{8,16},{16,24},{24,32},{32,40},{40,48},{48,56},{56,0},{1,9},... | collective-permute-start | bytes 147464 | tf_op jit(solution)/shard_map/ppermute | solution.py:532
  17.1 2.6 %collective-permute-start.5 = (f32[64,128]{1,0:T(8,128)S(1)}, f32[64,128]{1,0:T(8,128)S(1)}, u32[]{:S(2)}, u32[]{:S(2)}) collective-permute-start(f32[64,128]{1,0:T(8,128)S(1)} %plane.1), channel_id=1, source_target_pairs={{0,64},{64,128},{128,192},{192,0},{1,65},{65,129},{129,193},{193,1... | collective-permute-start | bytes 98312 | tf_op jit(solution)/shard_map/ppermute | solution.py:532

commit v5 on v4

--- a/solution.py
+++ b/solution.py
@@ -197,7 +197,7 @@
             for part in range(2):
                 for row in range(2):
                     for col in range(3):
-                        source = comp(direction, part, row, col)
+                        source = face_comp(direction, part, row, col)
                         target = face_comp(slot, part, row, col) * 4
                         if face == 0:
                             out[target : target + 4] = links[source, 0:DEPTHS]
@@ -209,7 +209,7 @@
                 target = ((part * 2 + row) * 3 + col) * 8
                 plane_out[target : target + 8] = packed(
                     [
-                        links[comp(direction, part, row, col), 8 * half : 8 * half + 8]
+                        links[face_comp(direction, part, row, col), 8 * half : 8 * half + 8]
                         for half in range(2)
                         for direction in OTHERS[2]
                     ],
@@ -365,7 +365,22 @@
     return jnp.where(right_edge, pltpu.roll(value, NX - 1, 1), pltpu.roll(value, LANES - 1, 1))
 
 
-def prepare_kernel(links, left, ahead, base):
+def prepare_kernel(pairs, links, left, ahead, base):
+    for direction in range(4):
+        for half in range(2):
+            rows = slice(8 * half, 8 * half + 8)
+            whole = [
+                [
+                    tuple(pairs[face_comp(direction, part, row, col), rows] for part in range(2))
+                    for col in range(3)
+                ]
+                for row in range(2)
+            ]
+            whole.append(third_row(whole[0], whole[1]))
+            for part in range(2):
+                for row in range(3):
+                    for col in range(3):
+                        links[comp(direction, part, row, col), rows] = whole[row][col][part]
     for part in range(2):
         for row in range(3):
             for col in range(3):
@@ -483,39 +498,40 @@
                 depth_out[at : at + 4] = value[4:8]
 
 
-def final_kernel(force, time_in, depth_in, plane_in, out, work):
+def final_kernel(force, time_in, depth_in, plane_in, out):
     first_plane = lax.broadcasted_iota(jnp.int32, (8, LANES), 1) < NX
+    row_at = row_index((8, LANES))
+    half_coeff = 0.5 * COEFF
+    upper = ((0, 1), (0, 2), (1, 2))
+
+    def total(direction, i, half):
+        value = force[direction * 8 + i, 8 * half : 8 * half + 8]
+        if direction != 2:
+            group = 3 * half + OTHERS[2].index(direction)
+            outer = unpacked(plane_in[8 * i : 8 * i + 8], group, False)
+            value = value - jnp.where(first_plane, outer, 0.0)
+        if direction != 0 and half == 0:
+            at = (OTHERS[0].index(direction) * 8 + i) * 4
+            later = time_in[at : at + 4]
+            value = value - jnp.concatenate([later, jnp.zeros_like(later)], axis=0)
+        if direction != 1:
+            at = (OTHERS[1].index(direction) * 8 + i) * 4 + 2 * half
+            value = value - jnp.where(row_at == 0, wide(depth_in, at), 0.0)
+            value = value - jnp.where(row_at == 4, wide(depth_in, at + 1), 0.0)
+        return value * half_coeff
+
     for direction in range(4):
-        for i in range(8):
-            c = direction * 8 + i
-            for half in range(2):
-                rows = slice(8 * half, 8 * half + 8)
-                total = force[c, rows]
-                if direction != 2:
-                    group = 3 * half + OTHERS[2].index(direction)
-                    outer = unpacked(plane_in[8 * i : 8 * i + 8], group, False)
-                    total = total - jnp.where(first_plane, outer, 0.0)
-                work[c, rows] = total
-            if direction != 0:
-                at = (OTHERS[0].index(direction) * 8 + i) * 4
-                work[c, 0:4] = work[c, 0:4] - time_in[at : at + 4]
-            if direction != 1:
-                at = (OTHERS[1].index(direction) * 8 + i) * 4
-                sites = pl.ds(0, TIMES, stride=DEPTHS)
-                work[c, sites] = work[c, sites] - depth_in[at : at + 4]
-        half_coeff = 0.5 * COEFF
-        upper = ((0, 1), (0, 2), (1, 2))
         for half in range(2):
             rows = slice(8 * half, 8 * half + 8)
             for n, (row, col) in enumerate(upper):
-                re = work[direction * 8 + 2 * n, rows] * half_coeff
-                im = work[direction * 8 + 2 * n + 1, rows] * half_coeff
+                re = total(direction, 2 * n, half)
+                im = total(direction, 2 * n + 1, half)
                 out[comp(direction, 0, row, col), rows] = re
                 out[comp(direction, 0, col, row), rows] = -re
                 out[comp(direction, 1, row, col), rows] = im
                 out[comp(direction, 1, col, row), rows] = im
-            d0 = work[direction * 8 + 6, rows] * half_coeff
-            d1 = work[direction * 8 + 7, rows] * half_coeff
+            d0 = total(direction, 6, half)
+            d1 = total(direction, 7, half)
             zero = jnp.zeros_like(d0)
             for k, value in enumerate((d0, d1, -(d0 + d1))):
                 out[comp(direction, 1, k, k), rows] = value
@@ -534,19 +550,24 @@
 
 
 def gauge_force(links):
-    flat = pltpu.with_memory_space_constraint(links.reshape(72, ROWS, LANES), pltpu.VMEM)
+    pairs = pltpu.with_memory_space_constraint(links[:, :, 0:2].reshape(48, ROWS, LANES), pltpu.VMEM)
     faces = pl.pallas_call(
         send_kernel, out_shape=(shape(144, LANES), shape(144, LANES), shape(96, LANES)), name="send"
-    )(flat)
+    )(pairs)
     depth = move(faces[1], "gz", False)
     time = move(faces[0], "ta", False)
     plane = move(faces[2], "gx", False)
-    local = pl.pallas_call(
+    flat, *local = pl.pallas_call(
         prepare_kernel,
-        out_shape=(shape(4, 12, 8, LANES), shape(4, 12, 8, LANES), shape(2, 18, 8, LANES)),
+        out_shape=(
+            shape(72, ROWS, LANES),
+            shape(4, 12, 8, LANES),
+            shape(4, 12, 8, LANES),
+            shape(2, 18, 8, LANES),
+        ),
         name="prepare",
-    )(flat)
-    local = [pltpu.with_memory_space_constraint(value, pltpu.VMEM) for value in local]
+    )(pairs)
+    flat, *local = [pltpu.with_memory_space_constraint(value, pltpu.VMEM) for value in (flat, *local)]
     sent = pl.pallas_call(faces_kernel, out_shape=(shape(96, LANES), shape(96, LANES)), name="faces")(
         *local, time, depth, plane
     )
@@ -568,7 +589,6 @@
     out = pl.pallas_call(
         final_kernel,
         out_shape=jax.ShapeDtypeStruct((72, ROWS, LANES), jnp.float32),
-        scratch_shapes=[pltpu.VMEM((32, ROWS, LANES), jnp.float32)],
         name="final",
     )(pltpu.with_memory_space_constraint(force, pltpu.VMEM), time, depth, plane)
     return out.reshape(links.shape)

time: 24.9 us -> 24.8 us (level)
    unnamed x4 -> x0, local copies, waits for them, and re-layouts: 1.25 us -> none
    slice x0 -> x1, local copies, waits for them, and re-layouts: none -> 1.02 us  [gauge_force(): links[:, :, 0:2].reshape(48, ROWS, LANES)]
where the time goes in v5:
time: 24.8 us; the launch traced here: 24.6 us
  starting transfers between devices  13.1 us (53%)
  waiting for transfers between devices  6.07 us (24%)
  Pallas kernels  4.42 us (18%)
  local copies, waits for them, and re-layouts  1.02 us (4%)
    ppermute x6, starting transfers between devices, move(): lax.ppermute(value, axis, [(i, (i + step) % count) for i in range(count)])  13.1 us
    ppermute x6, waiting for transfers between devices, move(): lax.ppermute(value, axis, [(i, (i + step) % count) for i in range(count)])  6.07 us
    pallas_call x1, Pallas kernels, gauge_force(): pl.pallas_call(interior_kernel, out_shape=shape(32, ROWS, LANES), scratch...  2.36 us
    slice x1, local copies, waits for them, and re-layouts, gauge_force(): links[:, :, 0:2].reshape(48, ROWS, LANES)  1.02 us
    pallas_call x1, Pallas kernels, gauge_force(): pl.pallas_call(final_kernel, out_shape=jax.ShapeDtypeStruct((72, ROWS, LA...  0.93 us
  transfers between devices with their start and end apart: 6, of which 3 were waited for; matrix products, arithmetic and copies ran while one was open for 0% of the time, Pallas kernels for 12%

profile of v5, /device:TPU:1, one launch (start us, length us, event | category | flops | bytes accessed | tf_op | source)
XLA Modules:
  0.0 24.6 jit_solution(2968685749857280133)
XLA Ops:
  0.0 1.0 %slice.3 = f32[4,2,2,3,4,4,128]{6,5,4,3,2,1,0:T(4,128)S(1)} slice(f32[4,2,3,3,4,4,128]{6,5,4,3,2,1,0:T(4,128)} %param.1), slice={[0:4], [0:2], [0:2], [0:3], [0:4], [0:4], [0:128]} | slice | bytes 786432 | tf_op jit(solution)/shard_map/slice | solution.py:553
  1.0 0.1 send.1
  1.2 6.5 %collective-permute-start = (f32[144,128]{1,0:T(8,128)S(1)}, f32[144,128]{1,0:T(8,128)S(1)}, u32[]{:S(2)}, u32[]{:S(2)}) collective-permute-start(f32[144,128]{1,0:T(8,128)S(1)} %get-tuple-element.15), channel_id=1, source_target_pairs={{0,7},{1,0},{2,1},{3,2},{4,3},{5,4},{6,5},{7,6},{8,15},{9,8},{10,9... | collective-permute-start | bytes 221192 | tf_op jit(solution)/shard_map/ppermute | solution.py:548
  7.6 5.1 %collective-permute-start.1 = (f32[144,128]{1,0:T(8,128)S(1)}, f32[144,128]{1,0:T(8,128)S(1)}, u32[]{:S(2)}, u32[]{:S(2)}) collective-permute-start(f32[144,128]{1,0:T(8,128)S(1)} %get-tuple-element.16), channel_id=1, source_target_pairs={{0,56},{8,0},{16,8},{24,16},{32,24},{40,32},{48,40},{56,48},{1,57}... | collective-permute-start | bytes 221192 | tf_op jit(solution)/shard_map/ppermute | solution.py:548
  12.7 1.2 %collective-permute-start.2 = (f32[96,128]{1,0:T(8,128)S(1)}, f32[96,128]{1,0:T(8,128)S(1)}, u32[]{:S(2)}, u32[]{:S(2)}) collective-permute-start(f32[96,128]{1,0:T(8,128)S(1)} %get-tuple-element.17), channel_id=1, source_target_pairs={{0,192},{64,0},{128,64},{192,128},{1,193},{65,1},{129,65},{193,129... | collective-permute-start | bytes 147464 | tf_op jit(solution)/shard_map/ppermute | solution.py:548
  14.0 0.4 %prepare.1 = (f32[72,16,128]{2,1,0:T(8,128)S(1)}, f32[4,12,8,128]{3,2,1,0:T(8,128)S(1)}, f32[4,12,8,128]{3,2,1,0:T(8,128)S(1)}, f32[2,18,8,128]{3,2,1,0:T(8,128)S(1)}) custom-call(f32[48,16,128]{2,1,0:T(8,128)S(1)} %bitcast.3), custom_call_target="tpu_custom_call" | custom-call | tf_op jit(solution)/shard_map/prepare/pallas_call | solution.py:560
  14.4 1.9 %collective-permute-done.2.plane_in = f32[96,128]{1,0:T(8,128)S(1)} collective-permute-done((f32[96,128]{1,0:T(8,128)S(1)}, f32[96,128]{1,0:T(8,128)S(1)}, u32[]{:S(2)}, u32[]{:S(2)}) %collective-permute-start.2) | collective-permute-done | bytes 49184 | tf_op jit(solution)/shard_map/ppermute | solution.py:548
  16.3 0.0 collective-permute-done.time_in
  16.3 0.0 collective-permute-done.1.depth_in
  16.3 0.4 %faces.1 = (f32[96,128]{1,0:T(8,128)S(1)}, f32[96,128]{1,0:T(8,128)S(1)}) custom-call(f32[4,12,8,128]{3,2,1,0:T(8,128)S(1)} %get-tuple-element.18.left, f32[4,12,8,128]{3,2,1,0:T(8,128)S(1)} %get-tuple-element.19.ahead, f32[2,18,8,128]{3,2,1,0:T(8,128)S(1)} %get-tuple-element.20.base, f32[144,128]{1,0:T(8,128)S(1)} %collective-permute-done.time_in, ...), custom_call_target="tpu_custom_call" | custom-call | tf_op jit(solution)/shard_map/faces/pallas_call | solution.py:571
  16.7 0.1 collective-permute-start.3
  16.8 0.1 collective-permute-start.4
  16.9 0.2 plane.1
  17.1 0.1 collective-permute-start.5
  17.1 2.4 %interior.1.force = f32[32,16,128]{2,1,0:T(8,128)S(1)} custom-call(f32[72,16,128]{2,1,0:T(8,128)S(1)} %get-tuple-element.14.links, f32[144,128]{1,0:T(8,128)S(1)} %collective-permute-done.time_in, f32[144,128]{1,0:T(8,128)S(1)} %collective-permute-done.1.depth_in, f32[96,128]{1,0:T(8,128)S(1)} %collective-permute-done.2.plane_in), custom_call_target="tpu_custom_call" | custom-call | tf_op jit(solution)/shard_map/interior/pallas_call | solution.py:577
  19.5 0.0 collective-permute-done.5.plane_in
  19.5 2.1 %collective-permute-done.3.time_in = f32[96,128]{1,0:T(8,128)S(1)} collective-permute-done((f32[96,128]{1,0:T(8,128)S(1)}, f32[96,128]{1,0:T(8,128)S(1)}, u32[]{:S(2)}, u32[]{:S(2)}) %collective-permute-start.3) | collective-permute-done | bytes 49184 | tf_op jit(solution)/shard_map/ppermute | solution.py:548
  21.6 2.1 %collective-permute-done.4.depth_in = f32[96,128]{1,0:T(8,128)S(1)} collective-permute-done((f32[96,128]{1,0:T(8,128)S(1)}, f32[96,128]{1,0:T(8,128)S(1)}, u32[]{:S(2)}, u32[]{:S(2)}) %collective-permute-start.4) | collective-permute-done | bytes 49184 | tf_op jit(solution)/shard_map/ppermute | solution.py:548
  23.7 0.9 %final.1 = f32[72,16,128]{2,1,0:T(8,128)} custom-call(f32[32,16,128]{2,1,0:T(8,128)S(1)} %interior.1.force, f32[96,128]{1,0:T(8,128)S(1)} %collective-permute-done.3.time_in, f32[96,128]{1,0:T(8,128)S(1)} %collective-permute-done.4.depth_in, f32[64,128]{1,0:T(8,128)S(1)} %collective-permute-done.5.plane_in), custom_call_target="tpu_custom_call" | custom-call | tf_op jit(solution)/shard_map/final/pallas_call | solution.py:589
Async XLA Ops:
  1.2 15.1 %collective-permute-start = (f32[144,128]{1,0:T(8,128)S(1)}, f32[144,128]{1,0:T(8,128)S(1)}, u32[]{:S(2)}, u32[]{:S(2)}) collective-permute-start(f32[144,128]{1,0:T(8,128)S(1)} %get-tuple-element.15), channel_id=1, source_target_pairs={{0,7},{1,0},{2,1},{3,2},{4,3},{5,4},{6,5},{7,6},{8,15},{9,8},{10,9... | collective-permute-start | bytes 221192 | tf_op jit(solution)/shard_map/ppermute | solution.py:548
  7.6 8.6 %collective-permute-start.1 = (f32[144,128]{1,0:T(8,128)S(1)}, f32[144,128]{1,0:T(8,128)S(1)}, u32[]{:S(2)}, u32[]{:S(2)}) collective-permute-start(f32[144,128]{1,0:T(8,128)S(1)} %get-tuple-element.16), channel_id=1, source_target_pairs={{0,56},{8,0},{16,8},{24,16},{32,24},{40,32},{48,40},{56,48},{1,57}... | collective-permute-start | bytes 221192 | tf_op jit(solution)/shard_map/ppermute | solution.py:548
  12.7 3.5 %collective-permute-start.2 = (f32[96,128]{1,0:T(8,128)S(1)}, f32[96,128]{1,0:T(8,128)S(1)}, u32[]{:S(2)}, u32[]{:S(2)}) collective-permute-start(f32[96,128]{1,0:T(8,128)S(1)} %get-tuple-element.17), channel_id=1, source_target_pairs={{0,192},{64,0},{128,64},{192,128},{1,193},{65,1},{129,65},{193,129... | collective-permute-start | bytes 147464 | tf_op jit(solution)/shard_map/ppermute | solution.py:548
  16.7 4.9 %collective-permute-start.3 = (f32[96,128]{1,0:T(8,128)S(1)}, f32[96,128]{1,0:T(8,128)S(1)}, u32[]{:S(2)}, u32[]{:S(2)}) collective-permute-start(f32[96,128]{1,0:T(8,128)S(1)} %get-tuple-element.21), channel_id=1, source_target_pairs={{0,1},{1,2},{2,3},{3,4},{4,5},{5,6},{6,7},{7,0},{8,9},{9,10},{10,1... | collective-permute-start | bytes 147464 | tf_op jit(solution)/shard_map/ppermute | solution.py:548
  16.8 6.9 %collective-permute-start.4 = (f32[96,128]{1,0:T(8,128)S(1)}, f32[96,128]{1,0:T(8,128)S(1)}, u32[]{:S(2)}, u32[]{:S(2)}) collective-permute-start(f32[96,128]{1,0:T(8,128)S(1)} %get-tuple-element.22), channel_id=1, source_target_pairs={{0,8},{8,16},{16,24},{24,32},{32,40},{40,48},{48,56},{56,0},{1,9},... | collective-permute-start | bytes 147464 | tf_op jit(solution)/shard_map/ppermute | solution.py:548
  17.1 2.5 %collective-permute-start.5 = (f32[64,128]{1,0:T(8,128)S(1)}, f32[64,128]{1,0:T(8,128)S(1)}, u32[]{:S(2)}, u32[]{:S(2)}) collective-permute-start(f32[64,128]{1,0:T(8,128)S(1)} %plane.1), channel_id=1, source_target_pairs={{0,64},{64,128},{128,192},{192,0},{1,65},{65,129},{129,193},{193,1... | collective-permute-start | bytes 98312 | tf_op jit(solution)/shard_map/ppermute | solution.py:548

commit v6 on v5

--- a/solution.py
+++ b/solution.py
@@ -101,7 +101,7 @@
 
 
 def plaquette(left, left_ahead, right, right_ahead):
-    first = product_rows(left[:2], left_ahead)
+    first = left if left_ahead is None else product_rows(left[:2], left_ahead)
     second = product_rows(right[:2], right_ahead)
     second.append(third_row(second[0], second[1]))
     loop = product_rows_dagger(first, second)
@@ -408,7 +408,6 @@
         ahead[0, at, 0:3] = links[comp(0, part, row, col), 13:16]
         ahead[0, at, 4:7] = links[comp(1, part, row, col), pl.ds(7, 3, stride=DEPTHS)]
         ahead[1, at] = turned(base[0, whole], 7)
-        ahead[2, at] = x_ahead(base[0, whole])
         c = comp(2, part, row, col)
         upper = links[c, 8:16]
         along_x = x_ahead(base[1, whole])
@@ -423,6 +422,20 @@
         ahead[3, at] = along_x
 
 
+    along = [
+        [tuple(x_ahead(base[0, part * 9 + row * 3 + col]) for part in range(2)) for col in range(3)]
+        for row in range(3)
+    ]
+    own = [
+        [tuple(left[2, face_comp(0, part, row, col)] for part in range(2)) for col in range(3)]
+        for row in range(2)
+    ]
+    for row, values in enumerate(product_rows(own, along)):
+        for col in range(3):
+            for part in range(2):
+                ahead[2, face_comp(0, part, row, col)] = values[col][part]
+
+
 def wide(ref, row):
     return jnp.broadcast_to(ref[row : row + 1], (8, LANES))
 
@@ -457,8 +470,6 @@
             depth_part = jnp.where(row_at % 2 == 1, wide(plane_in, at * 8 + 7), wide(plane_in, at * 8 + 3))
             depth_part = jnp.where(row_at < 6, turned(depth_part, 6), turned(depth_part, 3))
             return jnp.where(group == 7, jnp.where(row_at < 4, time_part, depth_part), own)
-        if unit == 2:
-            return own
         source = face_comp(1, part, row, col) * 4
         later = turned(time_in[source - 4 : source + 4], 4)
         own = jnp.where((group == 3) & (row_at >= 4), later, own)
@@ -480,12 +491,15 @@
             for row in range(3)
         ]
         own_left = [
-            [tuple(left[unit, face_comp(0, part, row, col)] for part in range(2)) for col in range(3)]
+            [
+                tuple((ahead if unit == 2 else left)[unit, face_comp(0, part, row, col)] for part in range(2))
+                for col in range(3)
+            ]
             for row in range(2)
         ]
         values = plaquette(
             own_left,
-            complete(lambda part, row, col: beside(unit, part, row, col)),
+            None if unit == 2 else complete(lambda part, row, col: beside(unit, part, row, col)),
             own_base,
             complete(lambda part, row, col: behind(unit, part, row, col)),
         )

time: 24.8 us -> 24.7 us (level)
  no operation moved by 1% of the time
where the time goes in v6:
time: 24.7 us; the launch traced here: 24.6 us
  starting transfers between devices  13.1 us (53%)
  waiting for transfers between devices  6.05 us (24%)
  Pallas kernels  4.41 us (18%)
  local copies, waits for them, and re-layouts  1.02 us (4%)
    ppermute x6, starting transfers between devices, move(): lax.ppermute(value, axis, [(i, (i + step) % count) for i in range(count)])  13.1 us
    ppermute x6, waiting for transfers between devices, move(): lax.ppermute(value, axis, [(i, (i + step) % count) for i in range(count)])  6.05 us
    pallas_call x1, Pallas kernels, gauge_force(): pl.pallas_call(interior_kernel, out_shape=shape(32, ROWS, LANES), scratch...  2.36 us
    slice x1, local copies, waits for them, and re-layouts, gauge_force(): links[:, :, 0:2].reshape(48, ROWS, LANES)  1.02 us
    pallas_call x1, Pallas kernels, gauge_force(): pl.pallas_call(final_kernel, out_shape=jax.ShapeDtypeStruct((72, ROWS, LA...  0.93 us
  transfers between devices with their start and end apart: 6, of which 3 were waited for; matrix products, arithmetic and copies ran while one was open for 0% of the time, Pallas kernels for 12%

profile of v6, /device:TPU:1, one launch (start us, length us, event | category | flops | bytes accessed | tf_op | source)
XLA Modules:
  0.0 24.6 jit_solution(9048124399471947924)
XLA Ops:
  0.0 1.0 %slice.3 = f32[4,2,2,3,4,4,128]{6,5,4,3,2,1,0:T(4,128)S(1)} slice(f32[4,2,3,3,4,4,128]{6,5,4,3,2,1,0:T(4,128)} %param.1), slice={[0:4], [0:2], [0:2], [0:3], [0:4], [0:4], [0:128]} | slice | bytes 786432 | tf_op jit(solution)/shard_map/slice | solution.py:567
  1.0 0.1 send.1
  1.2 6.5 %collective-permute-start = (f32[144,128]{1,0:T(8,128)S(1)}, f32[144,128]{1,0:T(8,128)S(1)}, u32[]{:S(2)}, u32[]{:S(2)}) collective-permute-start(f32[144,128]{1,0:T(8,128)S(1)} %get-tuple-element.15), channel_id=1, source_target_pairs={{0,7},{1,0},{2,1},{3,2},{4,3},{5,4},{6,5},{7,6},{8,15},{9,8},{10,9... | collective-permute-start | bytes 221192 | tf_op jit(solution)/shard_map/ppermute | solution.py:562
  7.6 5.1 %collective-permute-start.1 = (f32[144,128]{1,0:T(8,128)S(1)}, f32[144,128]{1,0:T(8,128)S(1)}, u32[]{:S(2)}, u32[]{:S(2)}) collective-permute-start(f32[144,128]{1,0:T(8,128)S(1)} %get-tuple-element.16), channel_id=1, source_target_pairs={{0,56},{8,0},{16,8},{24,16},{32,24},{40,32},{48,40},{56,48},{1,57}... | collective-permute-start | bytes 221192 | tf_op jit(solution)/shard_map/ppermute | solution.py:562
  12.7 1.2 %collective-permute-start.2 = (f32[96,128]{1,0:T(8,128)S(1)}, f32[96,128]{1,0:T(8,128)S(1)}, u32[]{:S(2)}, u32[]{:S(2)}) collective-permute-start(f32[96,128]{1,0:T(8,128)S(1)} %get-tuple-element.17), channel_id=1, source_target_pairs={{0,192},{64,0},{128,64},{192,128},{1,193},{65,1},{129,65},{193,129... | collective-permute-start | bytes 147464 | tf_op jit(solution)/shard_map/ppermute | solution.py:562
  14.0 0.4 %prepare.1 = (f32[72,16,128]{2,1,0:T(8,128)S(1)}, f32[4,12,8,128]{3,2,1,0:T(8,128)S(1)}, f32[4,12,8,128]{3,2,1,0:T(8,128)S(1)}, f32[2,18,8,128]{3,2,1,0:T(8,128)S(1)}) custom-call(f32[48,16,128]{2,1,0:T(8,128)S(1)} %bitcast.3), custom_call_target="tpu_custom_call" | custom-call | tf_op jit(solution)/shard_map/prepare/pallas_call | solution.py:574
  14.4 1.8 %collective-permute-done.2.plane_in = f32[96,128]{1,0:T(8,128)S(1)} collective-permute-done((f32[96,128]{1,0:T(8,128)S(1)}, f32[96,128]{1,0:T(8,128)S(1)}, u32[]{:S(2)}, u32[]{:S(2)}) %collective-permute-start.2) | collective-permute-done | bytes 49184 | tf_op jit(solution)/shard_map/ppermute | solution.py:562
  16.3 0.0 collective-permute-done.time_in
  16.3 0.0 collective-permute-done.1.depth_in
  16.3 0.4 %faces.1 = (f32[96,128]{1,0:T(8,128)S(1)}, f32[96,128]{1,0:T(8,128)S(1)}) custom-call(f32[4,12,8,128]{3,2,1,0:T(8,128)S(1)} %get-tuple-element.18.left, f32[4,12,8,128]{3,2,1,0:T(8,128)S(1)} %get-tuple-element.19.ahead, f32[2,18,8,128]{3,2,1,0:T(8,128)S(1)} %get-tuple-element.20.base, f32[144,128]{1,0:T(8,128)S(1)} %collective-permute-done.time_in, ...), custom_call_target="tpu_custom_call" | custom-call | tf_op jit(solution)/shard_map/faces/pallas_call | solution.py:585
  16.7 0.1 collective-permute-start.3
  16.7 0.1 collective-permute-start.4
  16.8 0.2 plane.1
  17.0 0.1 collective-permute-start.5
  17.1 2.4 %interior.1.force = f32[32,16,128]{2,1,0:T(8,128)S(1)} custom-call(f32[72,16,128]{2,1,0:T(8,128)S(1)} %get-tuple-element.14.links, f32[144,128]{1,0:T(8,128)S(1)} %collective-permute-done.time_in, f32[144,128]{1,0:T(8,128)S(1)} %collective-permute-done.1.depth_in, f32[96,128]{1,0:T(8,128)S(1)} %collective-permute-done.2.plane_in), custom_call_target="tpu_custom_call" | custom-call | tf_op jit(solution)/shard_map/interior/pallas_call | solution.py:591
  19.5 0.0 collective-permute-done.5.plane_in
  19.5 2.1 %collective-permute-done.3.time_in = f32[96,128]{1,0:T(8,128)S(1)} collective-permute-done((f32[96,128]{1,0:T(8,128)S(1)}, f32[96,128]{1,0:T(8,128)S(1)}, u32[]{:S(2)}, u32[]{:S(2)}) %collective-permute-start.3) | collective-permute-done | bytes 49184 | tf_op jit(solution)/shard_map/ppermute | solution.py:562
  21.5 2.1 %collective-permute-done.4.depth_in = f32[96,128]{1,0:T(8,128)S(1)} collective-permute-done((f32[96,128]{1,0:T(8,128)S(1)}, f32[96,128]{1,0:T(8,128)S(1)}, u32[]{:S(2)}, u32[]{:S(2)}) %collective-permute-start.4) | collective-permute-done | bytes 49184 | tf_op jit(solution)/shard_map/ppermute | solution.py:562
  23.7 0.9 %final.1 = f32[72,16,128]{2,1,0:T(8,128)} custom-call(f32[32,16,128]{2,1,0:T(8,128)S(1)} %interior.1.force, f32[96,128]{1,0:T(8,128)S(1)} %collective-permute-done.3.time_in, f32[96,128]{1,0:T(8,128)S(1)} %collective-permute-done.4.depth_in, f32[64,128]{1,0:T(8,128)S(1)} %collective-permute-done.5.plane_in), custom_call_target="tpu_custom_call" | custom-call | tf_op jit(solution)/shard_map/final/pallas_call | solution.py:603
Async XLA Ops:
  1.2 15.1 %collective-permute-start = (f32[144,128]{1,0:T(8,128)S(1)}, f32[144,128]{1,0:T(8,128)S(1)}, u32[]{:S(2)}, u32[]{:S(2)}) collective-permute-start(f32[144,128]{1,0:T(8,128)S(1)} %get-tuple-element.15), channel_id=1, source_target_pairs={{0,7},{1,0},{2,1},{3,2},{4,3},{5,4},{6,5},{7,6},{8,15},{9,8},{10,9... | collective-permute-start | bytes 221192 | tf_op jit(solution)/shard_map/ppermute | solution.py:562
  7.6 8.6 %collective-permute-start.1 = (f32[144,128]{1,0:T(8,128)S(1)}, f32[144,128]{1,0:T(8,128)S(1)}, u32[]{:S(2)}, u32[]{:S(2)}) collective-permute-start(f32[144,128]{1,0:T(8,128)S(1)} %get-tuple-element.16), channel_id=1, source_target_pairs={{0,56},{8,0},{16,8},{24,16},{32,24},{40,32},{48,40},{56,48},{1,57}... | collective-permute-start | bytes 221192 | tf_op jit(solution)/shard_map/ppermute | solution.py:562
  12.7 3.5 %collective-permute-start.2 = (f32[96,128]{1,0:T(8,128)S(1)}, f32[96,128]{1,0:T(8,128)S(1)}, u32[]{:S(2)}, u32[]{:S(2)}) collective-permute-start(f32[96,128]{1,0:T(8,128)S(1)} %get-tuple-element.17), channel_id=1, source_target_pairs={{0,192},{64,0},{128,64},{192,128},{1,193},{65,1},{129,65},{193,129... | collective-permute-start | bytes 147464 | tf_op jit(solution)/shard_map/ppermute | solution.py:562
  16.7 4.9 %collective-permute-start.3 = (f32[96,128]{1,0:T(8,128)S(1)}, f32[96,128]{1,0:T(8,128)S(1)}, u32[]{:S(2)}, u32[]{:S(2)}) collective-permute-start(f32[96,128]{1,0:T(8,128)S(1)} %get-tuple-element.21), channel_id=1, source_target_pairs={{0,1},{1,2},{2,3},{3,4},{4,5},{5,6},{6,7},{7,0},{8,9},{9,10},{10,1... | collective-permute-start | bytes 147464 | tf_op jit(solution)/shard_map/ppermute | solution.py:562
  16.7 6.9 %collective-permute-start.4 = (f32[96,128]{1,0:T(8,128)S(1)}, f32[96,128]{1,0:T(8,128)S(1)}, u32[]{:S(2)}, u32[]{:S(2)}) collective-permute-start(f32[96,128]{1,0:T(8,128)S(1)} %get-tuple-element.22), channel_id=1, source_target_pairs={{0,8},{8,16},{16,24},{24,32},{32,40},{40,48},{48,56},{56,0},{1,9},... | collective-permute-start | bytes 147464 | tf_op jit(solution)/shard_map/ppermute | solution.py:562
  17.0 2.5 %collective-permute-start.5 = (f32[64,128]{1,0:T(8,128)S(1)}, f32[64,128]{1,0:T(8,128)S(1)}, u32[]{:S(2)}, u32[]{:S(2)}) collective-permute-start(f32[64,128]{1,0:T(8,128)S(1)} %plane.1), channel_id=1, source_target_pairs={{0,64},{64,128},{128,192},{192,0},{1,65},{65,129},{129,193},{193,1... | collective-permute-start | bytes 98312 | tf_op jit(solution)/shard_map/ppermute | solution.py:562
